TPU v7x, 128 devices: a whole 4x4x4 slice. The times are simulated.
128 devices in a mesh: dp: 2 (over core), cp: 64 (over z, y, x).
Axes of the slice: x: 4, y: 4, z: 4, core: 2. Of those that a mesh axis runs over, the one named last changes fastest.
Arguments:
- inputs: bfloat16 [8, 16384, 322], P('dp', 'cp')
- latents: float32 [2048, 512], replicated
- x_gain: float32 [322], replicated
- x_shift: float32 [322], replicated
- z_gain: float32 [512], replicated
- z_shift: float32 [512], replicated
- w_query: bfloat16 [512, 512], replicated
- w_key: bfloat16 [322, 512], replicated
- w_value: bfloat16 [322, 512], replicated
- w_out: bfloat16 [512, 512], replicated
- m_gain: float32 [512], replicated
- m_shift: float32 [512], replicated
- w_up: bfloat16 [512, 512], replicated
- b_up: float32 [512], replicated
- w_down: bfloat16 [512, 512], replicated
- b_down: float32 [512], replicated
- d_out: bfloat16 [8, 2048, 512], P('dp')
Outputs:
- output 1: float32 [8, 2048, 512], P('dp')
- output 2: bfloat16 [8, 16384, 322], P('dp', 'cp')
- output 3: float32 [2048, 512], replicated
- output 4: float32 [322], replicated
- output 5: float32 [322], replicated
- output 6: float32 [512], replicated
- output 7: float32 [512], replicated
- output 8: float32 [512, 512], replicated
- output 9: float32 [322, 512], replicated
- output 10: float32 [322, 512], replicated
- output 11: float32 [512, 512], replicated
- output 12: float32 [512], replicated
- output 13: float32 [512], replicated
- output 14: float32 [512, 512], replicated
- output 15: float32 [512], replicated
- output 16: float32 [512, 512], replicated
- output 17: float32 [512], replicated
All inputs are finite; a program needn't handle non-finite values.
Results may differ from a plain program's by a relative error of at most 0.0176396.
Values sent between devices are 32-bit elements.
A program may use at most 1 GiB of HBM per device.

v0:
```python
import jax
import jax.numpy as jnp
from jax import lax
from jax.sharding import PartitionSpec as P

LN_EPS = 1e-5
LOW_TYPE = jnp.bfloat16
ACC_TYPE = jnp.float32


def layer_norm(tensor, ln_gain, ln_shift):
    row_mean = jnp.mean(tensor, axis=-1, keepdims=True)
    centred = tensor - row_mean
    variance = jnp.mean(centred * centred, axis=-1, keepdims=True)
    return centred * lax.rsqrt(variance + LN_EPS) * ln_gain + ln_shift


def contract(einsum_form, lhs_arr, rhs_arr):
    return jnp.einsum(einsum_form, lhs_arr, rhs_arr, preferred_element_type=ACC_TYPE)


def solution(mesh):
    x_spec = P('dp', 'cp', None)
    row_spec = P('dp', None, None)
    vec_spec = P(None)
    mat_spec = P(None, None)
    in_specs = (x_spec, mat_spec, vec_spec, vec_spec, vec_spec, vec_spec, mat_spec, mat_spec, mat_spec, mat_spec,
                vec_spec, vec_spec, mat_spec, vec_spec, mat_spec, vec_spec, row_spec)
    out_specs = (row_spec, x_spec, mat_spec, vec_spec, vec_spec, vec_spec, vec_spec, mat_spec, mat_spec, mat_spec, mat_spec,
                 vec_spec, vec_spec, mat_spec, vec_spec, mat_spec, vec_spec)

    def local_step(inputs, latents, x_gain, x_shift, z_gain, z_shift, w_query, w_key, w_value, w_out, m_gain, m_shift, w_up, b_up, w_down, b_down, d_out):
        qk_scale = w_query.shape[1] ** -0.5
        z_ln, z_pull = jax.vjp(layer_norm, latents, z_gain, z_shift)
        z_norm = z_ln.astype(LOW_TYPE)
        queries = contract('nd,dk->nk', z_norm, w_query).astype(LOW_TYPE)
        x_ln, x_pull = jax.vjp(layer_norm, inputs.astype(ACC_TYPE), x_gain, x_shift)
        x_norm = x_ln.astype(LOW_TYPE)
        key_rows = contract('bmc,ck->bmk', x_norm, w_key).astype(LOW_TYPE)
        value_rows = contract('bmc,cv->bmv', x_norm, w_value).astype(LOW_TYPE)
        logits = contract('nk,bmk->bnm', queries, key_rows) * qk_scale
        row_max = lax.pmax(jnp.max(logits, axis=-1, keepdims=True), 'cp')
        weights = jnp.exp(logits - row_max)
        row_sum, mixed_sum = lax.psum(
            (jnp.sum(weights, axis=-1, keepdims=True), contract('bnm,bmv->bnv', weights.astype(LOW_TYPE), value_rows)), 'cp')
        attn_out = (mixed_sum / row_sum).astype(LOW_TYPE)
        attn_probs = weights / row_sum
        z_mid = latents + contract('bnv,vd->bnd', attn_out, w_out)
        h_ln, h_pull = jax.vjp(layer_norm, z_mid, m_gain, m_shift)
        hidden = h_ln.astype(LOW_TYPE)
        act_f32, gelu_pull = jax.vjp(jax.nn.gelu, contract('bnd,de->bne', hidden, w_up) + b_up)
        act_val = act_f32.astype(LOW_TYPE)
        z_out = z_mid + contract('bne,ed->bnd', act_val, w_down) + b_down

        d_act = contract('bnd,ed->bne', d_out, w_down).astype(LOW_TYPE)
        (d_pre,) = gelu_pull(d_act.astype(ACC_TYPE))
        d_pre_low = d_pre.astype(LOW_TYPE)
        d_hidden = contract('bne,de->bnd', d_pre_low, w_up).astype(LOW_TYPE)
        d_mid_ln, d_m_gain_part, d_m_shift_part = h_pull(d_hidden.astype(ACC_TYPE))
        d_mid = d_out.astype(ACC_TYPE) + d_mid_ln
        d_mid_low = d_mid.astype(LOW_TYPE)
        d_attn = contract('bnd,vd->bnv', d_mid_low, w_out).astype(LOW_TYPE)
        mlp_grads = (
            contract('bnv,bnd->vd', attn_out, d_mid_low),
            d_m_gain_part, d_m_shift_part,
            contract('bnd,bne->de', hidden, d_pre_low),
            jnp.sum(d_pre, axis=(0, 1)),
            contract('bne,bnd->ed', act_val, d_out),
            jnp.sum(d_out.astype(ACC_TYPE), axis=(0, 1)),
            jnp.sum(d_mid, axis=0))
        d_w_out, d_m_gain, d_m_shift, d_w_up, d_b_up, d_w_down, d_b_down, d_mid_sum = lax.psum(mlp_grads, 'dp')

        d_probs = contract('bnv,bmv->bnm', d_attn, value_rows)
        row_dot = lax.psum(jnp.sum(attn_probs * d_probs, axis=-1, keepdims=True), 'cp')
        d_logits = (attn_probs * (d_probs - row_dot) * qk_scale).astype(LOW_TYPE)
        d_keys = contract('bnm,nk->bmk', d_logits, queries).astype(LOW_TYPE)
        d_values = contract('bnm,bnv->bmv', attn_probs.astype(LOW_TYPE), d_attn).astype(LOW_TYPE)
        d_x_norm = (contract('bmk,ck->bmc', d_keys, w_key) + contract('bmv,cv->bmc', d_values, w_value)).astype(LOW_TYPE)
        d_x_ln, d_x_gain_part, d_x_shift_part = x_pull(d_x_norm.astype(ACC_TYPE))
        d_query_part = contract('bnm,bmk->nk', d_logits, key_rows).astype(LOW_TYPE)
        shared_grads = (
            contract('nk,dk->nd', d_query_part, w_query),
            contract('nd,nk->dk', z_norm, d_query_part),
            contract('bmc,bmk->ck', x_norm, d_keys),
            contract('bmc,bmv->cv', x_norm, d_values),
            d_x_gain_part, d_x_shift_part)
        d_z_norm, d_w_query, d_w_key, d_w_value, d_x_gain, d_x_shift = lax.psum(shared_grads, ('dp', 'cp'))
        d_lat_ln, d_z_gain, d_z_shift = z_pull(d_z_norm)
        return (z_out, d_x_ln.astype(LOW_TYPE), d_lat_ln + d_mid_sum, d_x_gain, d_x_shift, d_z_gain, d_z_shift,
                d_w_query, d_w_key, d_w_value, d_w_out, d_m_gain, d_m_shift, d_w_up, d_b_up, d_w_down, d_b_down)

    return jax.shard_map(local_step, mesh=mesh, in_specs=in_specs, out_specs=out_specs, check_vma=False)
```

profile of v0, /device:TPU:1, one launch (start us, length us, event | category | flops | bytes accessed | tf_op | source)
XLA Modules:
  0.0 1492.0 jit_solution(16781193396875217488)
XLA Ops:
  27.3 296.4 %pmax.7 = f32[4,2048]{1,0:T(4,128)S(1)} all-reduce(f32[4,2048]{1,0:T(4,128)S(1)} %get-tuple-element.80), channel_id=1, replica_groups=mesh['dp'=2,'cp'=64] {'cp'}, use_global_device_ids=true, to_apply=%region_5.0 | all-reduce | flops 8192 | bytes 65536 | tf_op jit(solution)/shard_map/pmax | solution.py:42
  323.7 12.0 fusion.19
  341.1 11.5 copy.55
  357.4 288.6 %psum.120 = f32[4,2048]{1,0:T(4,128)S(1)} all-reduce(f32[4,2048]{1,0:T(4,128)S(1)} %fusion.17), channel_id=1, replica_groups=mesh['dp'=2,'cp'=64] {'cp'}, use_global_device_ids=true, to_apply=%region_8.0 | all-reduce | flops 8192 | bytes 65536 | tf_op jit(solution)/shard_map/psum | solution.py:44
  645.9 9.3 divide_convert_fusion
  655.9 15.0 %add_reduce_fusion = (f32[4,2048]{1,0:T(4,128)S(1)}, f32[4,2048,512]{1,2,0:T(8,128)}) fusion(f32[2048,512]{0,1:T(8,128)S(1)} %copy-done.5, bf16[4,2048,512]{2,1,0:T(8,128)(2,1)} %divide_convert_fusion, bf16[512,512]{1,0:T(8,128)(2,1)} %param.26), kind=kOutput, calls=%fused_computation.29 | convolution fusion | flops 4303347712 | bytes 29917184 | tf_op jit(solution)/shard_map/bnv,vd->bnd/dot_general | solution.py:19
  671.0 8.1 multiply_reduce_fusion
  685.6 8.2 fusion.51
  693.8 20.9 %fusion.72 = (f32[512]{0:T(512)}, bf16[4,2048,512]{2,1,0:T(8,128)(2,1)}) fusion(f32[4,2048,512]{2,1,0:T(8,128)} %fusion.51, f32[512]{0:T(512)S(1)} %copy-done.55, bf16[4,2048,512]{2,1,0:T(8,128)(2,1)} %param.33, bf16[512,512]{1,0:T(8,128)(2,1)S(1)} %copy-done.48), kind=kOutput, calls=%fused_computation.120 | convolution fusion | flops 4395630080 | bytes 34082816 | tf_op jit(solution)/shard_map/bnd,ed->bne/dot_general | solution.py:19
  714.7 15.3 %convert_reduce_fusion = (f32[512]{0:T(512)}, f32[4,2048]{1,0:T(4,128)S(1)}, bf16[4,2048,512]{1,2,0:T(8,128)(2,1)}) fusion(f32[512]{0:T(512)S(1)} %copy-done.40, f32[4,2048]{1,0:T(4,128)S(1)} %broadcast_multiply_fusion, f32[4,2048,512]{1,2,0:T(8,128)} %get-tuple-element.83, f32[2048,512]{0,1:T(8,128)S(1)} %copy-done.5, bf16[512,512]{1,0:T(8,128)(2,1)S(1)} %copy-done, ...), kind=kOutput, calls=%fused_computation.1 | convolution fusion | flops 4328513024 | bytes 38342656 | tf_op jit(solution)/shard_map/bne,de->bnd/dot_general | solution.py:19
  730.1 10.7 fusion.70
  740.8 23.4 %fusion.12 = (f32[512]{0:T(512)S(1)}, f32[2048,512]{0,1:T(8,128)}, f32[512]{0:T(512)S(1)}, bf16[4,2048,512]{1,2,0:T(8,128)(2,1)}) fusion(bf16[4,2048,512]{1,2,0:T(8,128)(2,1)S(1)} %copy-done.7, f32[4,2048,512]{1,2,0:T(8,128)} %get-tuple-element.83, f32[4,2048]{1,0:T(4,128)S(1)} %fusion.61, f32[4,2048]{1,0:T(4,128)S(1)} %broadcast_multiply_fusion, ...), kind=kLoop, calls=%fused_computation.22 | loop fusion | flops 70253568 | bytes 50468864 | tf_op jit(solution)/shard_map/transpose(jvp())/reduce_sum | solution.py:15
  764.2 11.4 convolution_bitcast_fusion.1
  775.7 7.4 convolution_convert_fusion
  789.9 12.4 multiply_reduce_fusion.1
  802.3 285.8 %psum.121 = f32[4,2048]{1,0:T(4,128)S(1)} all-reduce(f32[4,2048]{1,0:T(4,128)S(1)} %get-tuple-element.85), channel_id=1, replica_groups=mesh['dp'=2,'cp'=64] {'cp'}, use_global_device_ids=true, to_apply=%region_14.0 | all-reduce | flops 8192 | bytes 65536 | tf_op jit(solution)/shard_map/psum | solution.py:74
  1088.1 7.3 multiply_convert_fusion.1
  1115.5 11.2 fusion.38
  1126.7 14.1 convolution_bitcast_fusion
  1140.9 19.8 %add_add_fusion.1 = f32[4,2048,512]{1,2,0:T(8,128)} fusion(f32[4,2048,512]{1,2,0:T(8,128)} %get-tuple-element.83, f32[512]{0:T(512)S(1)} %copy-done.54, f32[2048,512]{0,1:T(8,128)} %copy.49, bf16[512,512]{1,0:T(8,128)(2,1)S(1)} %copy-done.49, f32[4,2048,512]{2,1,0:T(8,128)} %fusion.51, f32[512]{0:T(512)S(1)} %copy-done.55), kind=kOutput, calls=%fused_computation.23 | convolution fusion | flops 4349493248 | bytes 55054336 | tf_op jit(solution)/shard_map/bne,ed->bnd/dot_general | solution.py:19
  1160.7 16.4 %copy.63 = f32[4,2048,512]{2,1,0:T(8,128)} copy(f32[4,2048,512]{1,2,0:T(8,128)} %add_add_fusion.1) | data formatting | bytes 33554432
  1182.0 226.7 %all-reduce = (f32[322]{0:T(512)}, f32[322]{0:T(512)}) all-reduce(f32[322]{0:T(512)S(1)} %get-tuple-element.59, f32[322]{0:T(512)S(1)} %get-tuple-element.61), channel_id=1, replica_groups=mesh['dp'=2,'cp'=64] {'dp','cp'}, use_global_device_ids=true, to_apply=%region_23.0 | all-reduce | flops 644 | bytes 5152 | tf_op jit(solution)/shard_map/psum | solution.py:87
  1412.6 20.8 %all-reduce.10.cloned.1.call-done = (f32[2048,512]{1,0:T(8,128)}, f32[512,512]{1,0:T(8,128)}, f32[322,512]{1,0:T(8,128)}, f32[322,512]{1,0:T(8,128)}) async-done(((f32[2048,512]{1,0:T(8,128)}, f32[512,512]{1,0:T(8,128)}, f32[322,512]{1,0:T(8,128)}, f32[322,512]{1,0:T(8,128)}), (f32[2048,512]{1,0:T(8,128)}, f32[512,512]{1,0:T(8,128)}, f32[322,512]{1,0:T(8,128)}, ...) | async-done | bytes 6561808 | tf_op jit(solution)/shard_map/psum | solution.py:87
  1442.3 31.3 %all-reduce.12.cloned.1.call-done = (f32[2048,512]{1,0:T(8,128)}, f32[512,512]{1,0:T(8,128)}, f32[512,512]{1,0:T(8,128)}, f32[512,512]{1,0:T(8,128)}) async-done(((f32[2048,512]{1,0:T(8,128)}, f32[512,512]{1,0:T(8,128)}, f32[512,512]{1,0:T(8,128)}, f32[512,512]{1,0:T(8,128)}), (f32[2048,512]{1,0:T(8,128)}, f32[512,512]{1,0:T(8,128)}, f32[512,512]{1,0:T(8,128)}, ...) | async-done | bytes 7340048 | tf_op jit(solution)/shard_map/psum | solution.py:71
  (179 shorter events, 93.4 us)
Async XLA Ops:
  7.2 678.4 %copy-start = (bf16[512,512]{1,0:T(8,128)(2,1)S(1)}, bf16[512,512]{1,0:T(8,128)(2,1)}, u32[]{:S(2)}) copy-start(bf16[512,512]{1,0:T(8,128)(2,1)} %param.29) | copy-start | bytes 1572868
  7.3 638.7 %all-reduce.8.cloned.1.call-start = ((), (), s32[]{:S(2)}) async-start(), calls=%async_computation | async-start | bytes 33554432 | tf_op jit(solution)/shard_map/psum | solution.py:44
  17.2 306.5 %copy-start.14 = (bf16[4,256,512]{2,1,0:T(8,128)(2,1)}, bf16[4,256,512]{2,1,0:T(8,128)(2,1)S(1)}, u32[]{:S(2)}) copy-start(bf16[4,256,512]{2,1,0:T(8,128)(2,1)S(1)} %convolution_convert_fusion.3) | copy-start | bytes 3145732
  335.7 1097.7 %all-reduce.10.cloned.1.call-start = ((), (), s32[]{:S(2)}) async-start(), calls=%async_computation.1 | async-start | bytes 13172736 | tf_op jit(solution)/shard_map/psum | solution.py:87
  740.8 42.2 %slice-start = ((s8[8388608]{0:T(1024)(128)(4,1)}), s8[4194304]{0:T(1024)(128)(4,1)S(1)}, s32[]{:S(2)}) async-start(s8[8388608]{0:T(1024)(128)(4,1)} %bitcast.97), calls=%async_computation.3 | async-start | bytes 8388608
  764.2 11.4 copy-start.11
  764.2 11.4 copy-start.47
  764.2 18.8 %slice-start.1 = ((s8[8388608]{0:T(1024)(128)(4,1)}), s8[4194304]{0:T(1024)(128)(4,1)S(1)}, s32[]{:S(2)}) async-start(s8[8388608]{0:T(1024)(128)(4,1)} %bitcast.97), calls=%async_computation.4 | async-start | bytes 8388608
  1115.5 358.1 %all-reduce.12.cloned.1.call-start = ((), (), s32[]{:S(2)}) async-start(), calls=%async_computation.2 | async-start | bytes 14680064 | tf_op jit(solution)/shard_map/psum | solution.py:71
  1126.7 14.1 copy-start.49
  1126.7 14.1 copy-start.54
  1160.7 16.4 %copy-start.25 = (bf16[322,512]{1,0:T(8,128)(2,1)S(1)}, bf16[322,512]{1,0:T(8,128)(2,1)}, u32[]{:S(2)}) copy-start(bf16[322,512]{1,0:T(8,128)(2,1)} %param.24) | copy-start | bytes 989188
  1160.7 17.0 %copy-start.51 = (bf16[322,512]{1,0:T(8,128)(2,1)S(1)}, bf16[322,512]{1,0:T(8,128)(2,1)}, u32[]{:S(2)}) copy-start(bf16[322,512]{1,0:T(8,128)(2,1)} %param.25) | copy-start | bytes 989188
  1160.7 19.0 %copy-start.37 = (f32[4,256]{1,0:T(4,128)S(1)}, f32[4,256]{1,0:T(4,128)}, u32[]{:S(2)}) copy-start(f32[4,256]{1,0:T(4,128)} %copy-done.36) | copy-start | bytes 12292
  1177.1 231.7 %copy-start.45 = (f32[512]{0:T(512)S(1)}, f32[512]{0:T(512)}, u32[]{:S(2)}) copy-start(f32[512]{0:T(512)} %get-tuple-element.88) | copy-start | bytes 6148
  1177.1 231.7 %copy-start.46 = (f32[512]{0:T(512)S(1)}, f32[512]{0:T(512)}, u32[]{:S(2)}) copy-start(f32[512]{0:T(512)} %get-tuple-element.56) | copy-start | bytes 6148
  1177.1 256.3 %copy-start.27 = (f32[2048]{0:T(1024)S(1)}, f32[2048]{0:T(1024)}, u32[]{:S(2)}) copy-start(f32[2048]{0:T(1024)} %copy-done.26) | copy-start | bytes 24580
  1177.1 256.3 %copy-start.29 = (f32[2048]{0:T(1024)S(1)}, f32[2048]{0:T(1024)}, u32[]{:S(2)}) copy-start(f32[2048]{0:T(1024)} %copy-done.28) | copy-start | bytes 24580
  1177.1 256.3 %copy-start.39 = (f32[512]{0:T(512)S(1)}, f32[512]{0:T(512)}, u32[]{:S(2)}) copy-start(f32[512]{0:T(512)} %param.21) | copy-start | bytes 6148
  1177.7 260.9 %copy-start.31 = (f32[2048]{0:T(1024)S(1)}, f32[2048]{0:T(1024)}, u32[]{:S(2)}) copy-start(f32[2048]{0:T(1024)} %copy-done.30) | copy-start | bytes 24580
  1442.2 37.4 %copy-start.16 = (f32[512,512]{1,0:T(8,128)S(1)}, f32[512,512]{1,0:T(8,128)}, u32[]{:S(2)}) copy-start(f32[512,512]{1,0:T(8,128)} %get-tuple-element.99) | copy-start | bytes 3145732
  1442.2 38.4 %copy-start.21 = (f32[322,512]{1,0:T(8,128)S(1)}, f32[322,512]{1,0:T(8,128)}, u32[]{:S(2)}) copy-start(f32[322,512]{1,0:T(8,128)} %get-tuple-element.100) | copy-start | bytes 1978372
  1442.2 39.2 %copy-start.20 = (f32[322,512]{1,0:T(8,128)S(1)}, f32[322,512]{1,0:T(8,128)}, u32[]{:S(2)}) copy-start(f32[322,512]{1,0:T(8,128)} %get-tuple-element.101) | copy-start | bytes 1978372
  1473.6 11.7 copy-start.1
  (41 other events, 309.8 us)
Sparse Core Ops, SparseCore 0:
  335.8 262.7 all-reduce.7
  1115.6 317.7 all-reduce.9
  1437.4 36.0 all-reduce.11
where the time goes:
time: 1500 us; the launch traced here: 1490 us
  blocking collectives  1100 us (73%)
  matrix products  180 us (12%)
  other arithmetic  91.9 us (6%)
  waiting for transfers between devices  52.2 us (3%)
  local copies, waits for them, and re-layouts  51.4 us (3%)
    pmax x1, blocking collectives, local_step(): row_max = lax.pmax(jnp.max(logits, axis=-1, keepdims=True), 'cp')  296 us
    psum x1, blocking collectives, local_step(): lax.psum((jnp.sum(weights, axis=-1, keepdims=True), contract('bnm,bmv->bn...  289 us
    psum x1, blocking collectives, local_step(): lax.psum(jnp.sum(attn_probs * d_probs, axis=-1, keepdims=True), 'cp')  286 us
    psum x1, blocking collectives, local_step(): lax.psum(shared_grads, ('dp', 'cp'))  227 us
    dot_general x24, matrix products, contract(): jnp.einsum(einsum_form, lhs_arr, rhs_arr, preferred_element_type=ACC_TYPE)  180 us
    unnamed x134, local copies, waits for them, and re-layouts  46 us
    psum x1, waiting for transfers between devices, local_step(): lax.psum(mlp_grads, 'dp')  31.3 us
  transfers between devices with their start and end apart: 3, of which 2 were waited for; matrix products, arithmetic and copies ran while one was open for 6% of the time, Pallas kernels for 0%

commit v1 on v0

v1 whole, which is shorter than its diff:
```python
import functools
import math

import jax
import jax.numpy as jnp
from jax import lax
from jax.experimental import pallas as pl
from jax.experimental.pallas import tpu as pltpu
from jax.sharding import PartitionSpec as P

LN_EPS = 1e-5
BF16 = jnp.bfloat16
F32 = jnp.float32
MESH_ID = pl.DeviceIdType.MESH
SIDE = 4
PLANE = SIDE * SIDE
LANES = 128
LATENT_TILE = 256
LOG2E = math.log2(math.e)
GELU_C = math.sqrt(2.0 / math.pi)
GELU_A = 0.044715
HALF_TILES = 20
STREAM_TILES = ((0, 7), (7, 14), (14, 20))
STREAM_ROWS = ((0, 32), (32, 80), (80, 128))
VMEM_LIMIT = 67043328
STREAM_AXES = ((2, 1, 0), (1, 0, 2), (0, 2, 1))


def contract(form, lhs, rhs):
    return jnp.einsum(form, lhs, rhs, preferred_element_type=F32)


def dot(lhs, rhs, dims):
    return lax.dot_general(lhs, rhs, (dims, ((), ())), preferred_element_type=F32)


NN = ((1,), (0,))
NT = ((1,), (1,))
TN = ((0,), (0,))
DOWN, ACROSS = 0, 1
HOPS = (2, 1, 3)


def mean(value, axis=ACROSS):
    return jnp.mean(value, axis=axis, keepdims=True)


def total(value, axis=DOWN):
    return jnp.sum(value, axis=axis, keepdims=True)


def zeros(*shape):
    return jnp.zeros(shape, F32)


def lanes(t):
    return pl.ds(t * LANES, LANES)


def tile_rows(i, size):
    return pl.ds(pl.multiple_of(i * size, size), size)


def norm_parts(value, axis=ACROSS):
    centred = value - mean(value, axis)
    rstd = lax.rsqrt(mean(centred * centred, axis) + LN_EPS)
    return centred * rstd, rstd


def norm_pull(d_normed, unit, rstd, gain, axis=ACROSS):
    d_unit = d_normed * gain
    return rstd * (d_unit - mean(d_unit, axis) - unit * mean(d_unit * unit, axis))


def row_pair(ref, i):
    return jnp.concatenate([ref[pl.ds(2 * i, 1), :], ref[pl.ds(2 * i + 1, 1), :]], axis=ACROSS)


def sum_slots(ref, *index):
    return ref[(0,) + index] + ref[(1,) + index] + ref[(2,) + index]


def gelu_parts(pre):
    tanh = jnp.tanh(GELU_C * (pre + GELU_A * pre * pre * pre))
    slope = 0.5 * (1.0 + tanh) + 0.5 * pre * (1.0 - tanh * tanh) * (GELU_C * (1.0 + 3.0 * GELU_A * pre * pre))
    return 0.5 * pre * (1.0 + tanh), slope


def chip_coords():
    cp = lax.axis_index('cp')
    return lax.div(cp, PLANE), lax.rem(lax.div(cp, SIDE), SIDE), lax.rem(cp, SIDE)


def chip(z, y, x):
    return {'cp': z * PLANE + y * SIDE + x}


def moved(coords, axis, offset):
    shifted = list(coords)
    shifted[axis] = lax.rem(coords[axis] + offset + SIDE, SIDE)
    return tuple(shifted)


def enter(peers):
    barrier = pltpu.get_barrier_semaphore()
    for peer in peers:
        pl.semaphore_signal(barrier, inc=1, device_id=peer, device_id_type=MESH_ID)
    pl.semaphore_wait(barrier, len(peers))


class Copies:
    def __init__(self, send_sems, recv_sems):
        self.send_sems, self.recv_sems, self.used, self.open = send_sems, recv_sems, 0, []

    def start(self, src, dst, peer):
        copy = pltpu.make_async_remote_copy(
            src_ref=src, dst_ref=dst, send_sem=self.send_sems.at[self.used], recv_sem=self.recv_sems.at[self.used],
            device_id=peer, device_id_type=MESH_ID)
        self.used += 1
        copy.start()
        self.open.append(copy)
        return copy

    def sent(self, copy):
        copy.wait_send()
        self.open = [other for other in self.open if other is not copy]

    def finish(self):
        for copy in self.open:
            copy.wait_send()


def forward_kernel(
        x_blocks, latents, x_gain, x_shift, z_gain, z_shift, w_query, w_key, w_value,
        z0, d_out, w_out, w_up, w_down, m_gain, m_shift, b_up, b_down,
        q, k, v, x_in, z_out, d_attn_all, stats_all, top_all, d_mid_out, w_grads, vec_grads,
        vt, logits, mixed, top_own, tops, sum_own, sum_parts, sums, ra1, rb1, pa1, pb1, ra2, rb2, d_attn_f32, stats_f32,
        send_sems, recv_sems):
    me = chip_coords()
    z, y, x = me
    owner = y * SIDE + x
    plane_peers = []
    for d in range(1, PLANE):
        other = lax.rem(owner + d, PLANE)
        plane_peers.append((other, chip(z, lax.div(other, SIDE), lax.rem(other, SIDE))))
    enter([device for _, device in plane_peers] + [chip(*moved(me, 0, d)) for d in HOPS])
    copies = Copies(send_sems, recv_sems)
    qk_scale = q.shape[1] ** -0.5
    to_log2 = qk_scale * LOG2E
    tiles = q.shape[0] // LATENT_TILE
    half_v = vt.shape[0] // 2
    block_rows = x_blocks.shape[-1]

    got_x = {}
    for d in HOPS:
        peer = moved(me, 0, d)
        got_x[d] = copies.start(x_blocks.at[peer[0]], x_in.at[z], chip(*peer))
    x_in[z] = x_blocks[z]
    top_own[...] = jnp.full(top_own.shape, -jnp.inf, F32)

    def query_tile(i, carry):
        rows = tile_rows(i, LATENT_TILE)
        unit, _ = norm_parts(latents[rows, :])
        z_norm = (unit * z_gain[...] + z_shift[...]).astype(BF16)
        q[rows, :] = dot(z_norm, w_query[...], NN).astype(BF16)
        return carry

    lax.fori_loop(0, tiles, query_tile, 0)

    def block_logits(j):
        rows = tile_rows(j, block_rows)
        unit, _ = norm_parts(x_in[j], DOWN)
        x_norm = (unit * x_gain[...] + x_shift[...]).astype(BF16)
        k[rows, :] = dot(x_norm, w_key[...], TN).astype(BF16)
        v[rows, :] = dot(x_norm, w_value[...], TN).astype(BF16)
        vt[:, rows] = dot(w_value[...], x_norm, TN).astype(BF16)

        def logits_tile(i, carry):
            s = dot(k[rows, :], q[tile_rows(i, LATENT_TILE), :], NT)
            logits[i, rows, :] = s
            top = jnp.max(s, axis=DOWN, keepdims=True)
            for h in range(2):
                row = pl.ds(2 * i + h, 1)
                top_own[row, :] = jnp.maximum(top_own[row, :], top[:, h * LANES:(h + 1) * LANES])
            return carry

        lax.fori_loop(0, tiles, logits_tile, 0)

    block_logits(z)
    for d in HOPS[::-1]:
        got_x[d].wait_recv()
        block_logits(moved(me, 0, -d)[0])
    top_own[...] = jnp.ceil(top_own[...] * to_log2)
    tops[owner] = top_own[...]
    top_copies = [copies.start(top_own, tops.at[owner], device) for _, device in plane_peers]

    def mix_tile(i, carry):
        top = row_pair(top_own, i)
        w = jnp.exp2(logits[i] * to_log2 - top)
        weight_sum = total(w)
        for h in range(2):
            sum_own[pl.ds(2 * i + h, 1), :] = weight_sum[:, h * LANES:(h + 1) * LANES]
        product = dot(vt[...], w.astype(BF16), NN)
        at_y, at_x = lax.div(i, 2), 2 * lax.rem(i, 2)
        for h in range(2):
            mixed[at_y, at_x + h] = product[:, h * LANES:(h + 1) * LANES]
        return carry

    lax.fori_loop(0, tiles, mix_tile, 0)
    for copy in top_copies:
        copy.wait_recv()
    top = functools.reduce(jnp.maximum, [tops[i] for i in range(PLANE)])
    top_all[...] = top
    factor = jnp.exp2(top_own[...] - top)
    scaled_sum = sum_own[...] * factor
    for i in range(PLANE):
        mixed[i // SIDE, i % SIDE] = mixed[i // SIDE, i % SIDE] * factor[i:i + 1, :]
        sum_parts[i] = jnp.broadcast_to(scaled_sum[i:i + 1, :], (8, LANES))

    first = [[], []]
    for d in HOPS:
        peer = moved(me, 2, d)
        first[0].append(copies.start(mixed.at[:, peer[2], 0:half_v, :], ra1.at[d - 1], chip(*peer)))
        peer = moved(me, 1, d)
        first[1].append(copies.start(mixed.at[peer[1], :, half_v:2 * half_v, :], rb1.at[d - 1], chip(*peer)))
    sums[owner] = sum_parts[owner]
    sum_copies = [copies.start(sum_parts.at[other], sums.at[owner], device) for other, device in plane_peers]
    for copy in first[0]:
        copy.wait_recv()
    second = [[], []]
    for i in range(SIDE):
        pa1[i] = mixed[i, x, 0:half_v, :] + sum_slots(ra1, i)
    for d in HOPS:
        peer = moved(me, 1, d)
        second[0].append(copies.start(pa1.at[peer[1]], ra2.at[d - 1], chip(*peer)))
    for copy in first[1]:
        copy.wait_recv()
    for i in range(SIDE):
        pb1[i] = mixed[y, i, half_v:2 * half_v, :] + sum_slots(rb1, i)
    for d in HOPS:
        peer = moved(me, 2, d)
        second[1].append(copies.start(pb1.at[peer[2]], rb2.at[d - 1], chip(*peer)))
    for copy in sum_copies:
        copy.wait_recv()
    inv_sum = 1.0 / functools.reduce(lambda a, b: a + b, [sums[i] for i in range(PLANE)])
    for copy in second[0] + second[1]:
        copy.wait_recv()
    upper = pa1[y] + sum_slots(ra2)
    lower = pb1[x] + sum_slots(rb2)
    attn_t = jnp.concatenate([upper, lower], axis=DOWN) * inv_sum[0:1, :]

    attn_t_low = attn_t.astype(BF16)
    attn_low = attn_t.T.astype(BF16)
    z_mid = z0[...] + dot(attn_low, w_out[...], NN)
    unit, rstd = norm_parts(z_mid)
    hidden_f32 = unit * m_gain[...] + m_shift[...]
    hidden = hidden_f32.astype(BF16)
    pre = dot(hidden, w_up[...], NN) + b_up[...]
    act_f32, slope = gelu_parts(pre)
    act = act_f32.astype(BF16)
    z_out[...] = z_mid + dot(act, w_down[...], NN) + b_down[...]

    d_out_low = d_out[...]
    d_out_f32 = d_out_low.astype(F32)
    d_act = dot(d_out_low, w_down[...], NT).astype(BF16).astype(F32)
    d_pre = d_act * slope
    d_pre_low = d_pre.astype(BF16)
    d_hidden = dot(d_pre_low, w_up[...], NT).astype(BF16).astype(F32)
    d_mid = d_out_f32 + norm_pull(d_hidden, unit, rstd, m_gain[...])
    d_mid_low = d_mid.astype(BF16)
    d_attn = dot(d_mid_low, w_out[...], NT).astype(BF16).astype(F32)
    row_dot = total(d_attn.T * attn_t)

    half_r = LANES // 2
    d_attn_f32[y, x] = d_attn
    stats_f32[owner, 0:1, :] = row_dot
    stats_f32[owner, 1:2, :] = inv_sum[0:1, :]
    up, down = pl.ds(0, half_r), pl.ds(half_r, half_r)
    first = [[], []]
    for d in HOPS:
        first[0].append(copies.start(d_attn_f32.at[y, x, up], d_attn_f32.at[y, x, up], chip(*moved(me, 1, d))))
        first[1].append(copies.start(d_attn_f32.at[y, x, down], d_attn_f32.at[y, x, down], chip(*moved(me, 2, d))))
    stat_copies = [copies.start(stats_f32.at[owner], stats_f32.at[owner], device) for _, device in plane_peers]

    d_mid_out[...] = d_mid
    w_grads[0] = dot(attn_t_low, d_mid_low, NN)
    w_grads[1] = dot(hidden_f32.T.astype(BF16), d_pre_low, NN)
    w_grads[2] = dot(act_f32.T.astype(BF16), d_out_low, NN)
    for i, value in enumerate((d_hidden * unit, d_hidden, d_pre, d_out_f32)):
        vec_grads[i:i + 1, :] = total(value)
    vec_grads[4:8, :] = zeros(4, vec_grads.shape[1])

    second = []
    for copy in first[0]:
        copy.wait_recv()
    for d in HOPS:
        second.append(copies.start(d_attn_f32.at[:, x, up], d_attn_f32.at[:, x, up], chip(*moved(me, 2, d))))
    for copy in first[1]:
        copy.wait_recv()
    for d in HOPS:
        second.append(copies.start(d_attn_f32.at[y, :, down], d_attn_f32.at[y, :, down], chip(*moved(me, 1, d))))
    for copy in stat_copies + second:
        copy.wait_recv()
    copies.finish()
    stats_all[...] = stats_f32[...]
    for i in range(PLANE):
        d_attn_all[i] = d_attn_f32[i // SIDE, i % SIDE].astype(BF16)


def forward_block(x_blocks, latents, *others, collective_id):
    latents_n, width = latents.shape
    _, channels, block_rows = x_blocks.shape
    elements = SIDE * block_rows
    chunk = latents_n // PLANE
    half = width // 2
    vmem = pl.BlockSpec(memory_space=pltpu.VMEM)
    n_copies = 3 * PLANE + 24
    shape, wide = jax.ShapeDtypeStruct, pltpu.VMEM
    stat, slots = (PLANE, 8, LANES), (3, SIDE, half, LANES)
    return pl.pallas_call(
        forward_kernel,
        out_shape=(
            shape((latents_n, width), BF16), shape((elements, width), BF16), shape((elements, width), BF16),
            shape(x_blocks.shape, F32), shape((chunk, width), F32), shape((PLANE, chunk, width), BF16),
            shape(stat, F32), shape((PLANE, LANES), F32), shape((chunk, width), F32), shape((3, width, width), F32),
            shape((8, width), F32)),
        in_specs=[vmem] * (2 + len(others)),
        out_specs=(vmem,) * 11,
        scratch_shapes=[
            wide((width, elements), BF16), wide((latents_n // LATENT_TILE, elements, LATENT_TILE), F32),
            wide((SIDE, SIDE, width, LANES), F32),
            wide((PLANE, LANES), F32), wide((PLANE, PLANE, LANES), F32), wide((PLANE, LANES), F32), wide(stat, F32), wide(stat, F32),
            wide(slots, F32), wide(slots, F32), wide(slots[1:], F32), wide(slots[1:], F32),
            wide((3, half, LANES), F32), wide((3, half, LANES), F32),
            wide((SIDE, SIDE, chunk, width), F32), wide(stat, F32),
            pltpu.SemaphoreType.DMA((n_copies,)), pltpu.SemaphoreType.DMA((n_copies,))],
        compiler_params=pltpu.CompilerParams(
            collective_id=collective_id, has_side_effects=True, vmem_limit_bytes=VMEM_LIMIT),
    )(x_blocks, latents, *others)


def at(free, coords, **other):
    index = []
    for axis, name in enumerate('zyx'):
        index.append(other[name] if name in other else (slice(None) if axis in free else coords[axis]))
    return tuple(index)


def on(axis, value):
    return {'zyx'[axis]: value}


def tile_place(t):
    return t // HALF_TILES, t % HALF_TILES


def backward_kernel(
        q, k, v, d_attn, stats, top, z_rows, d_mid, vec_grads, x_gain, x_shift, z_gain, z_shift, w_query, w_key, w_value,
        w_grads, x_in, latents_in,
        z_all, d_inputs, d_lat_out, w_out_grads, kv_out, vec_out,
        probs, d_logits, d_q, d_k, d_v, x_rows, x_norm, x_sums, d_x, d_x_in, latents, z_norm, vecs, g, core_in, *rest):
    n, per = len(STREAM_TILES), 8
    side_in = [rest[per * s:per * s + 2] for s in range(n)]
    full_in = [rest[per * s + 2:per * s + 4] for s in range(n)]
    recvs = [(None,) + rest[per * s + 4:per * s + 6] for s in range(n)]
    parts = [rest[per * s + 6:per * s + 8] for s in range(n)]
    send_sems, recv_sems, local_sems, half_free = rest[per * n:]
    me = chip_coords()
    z, y, x = me
    dp = lax.axis_index('dp')
    partner = {'dp': 1 - dp}
    qk_scale = q.shape[1] ** -0.5
    to_log2 = qk_scale * LOG2E
    width = q.shape[1]
    channels = x_rows.shape[1]
    halves = (slice(0, SIDE // 2), slice(SIDE // 2, SIDE))
    tiles = q.shape[0] // LATENT_TILE
    split = width // LANES
    chips = SIDE ** 3

    local = []

    def fetch(src, dst):
        copy = pltpu.make_async_copy(src, dst, local_sems.at[len(local)])
        copy.start()
        local.append(copy)
        return copy

    enter([partner] + [chip(*moved(me, axis, d)) for axis in range(3) for d in HOPS])
    copies = Copies(send_sems, recv_sems)

    own_z = fetch(z_rows, z_all.at[z, y, x])
    z_pending = []
    for s, (lo, hi) in enumerate(STREAM_ROWS):
        rows = pl.ds(lo, hi - lo)
        z_pending.append([
            copies.start(z_rows.at[rows], z_all.at[z, y, x, rows], chip(*moved(me, STREAM_AXES[s][0], d))) for d in HOPS])
    got_x = fetch(x_in, x_rows)
    got_latents = fetch(latents_in, latents)
    got_w = []
    for i in range(3):
        for t in range(split):
            half, slot = tile_place(20 + split * i + t)
            got_w.append(fetch(w_grads.at[i, :, :, :, :, lanes(t)], g.at[half, :, :, :, slot]))
    x_norm[...] = jnp.zeros(x_norm.shape, BF16)

    def pair(ref, i, row):
        return jnp.concatenate([ref[2 * i + h, row:row + 1, :] for h in range(2)], axis=ACROSS)

    def attend_tile(i, carry):
        rows = tile_rows(i, LATENT_TILE)
        peak = row_pair(top, i)
        row_dot, inv_sum = pair(stats, i, 0), pair(stats, i, 1)
        p = jnp.exp2(dot(k[...], q[rows, :], NT) * to_log2 - peak) * inv_sum
        probs[:, rows] = p.astype(BF16)
        d_p = dot(v[...], d_attn[rows, :], NT)
        d_s = (p * (d_p - row_dot) * qk_scale).astype(BF16)
        d_logits[:, rows] = d_s
        d_q[rows, :] = dot(d_s, k[...], TN).astype(BF16)
        return carry

    lax.fori_loop(0, tiles // 2, attend_tile, 0)
    own_z.wait()
    for s, (lo, hi) in enumerate(STREAM_ROWS):
        for copy in z_pending[s]:
            copy.wait_recv()
        first, second, _ = STREAM_AXES[s]
        ref = z_all.at[at((first,), me) + (pl.ds(lo, hi - lo),)]
        z_pending[s] = [copies.start(ref, ref, chip(*moved(me, second, d))) for d in (1, -1)]
    lax.fori_loop(tiles // 2, tiles, attend_tile, 0)

    for s, (lo, hi) in enumerate(STREAM_ROWS):
        first, second, _ = STREAM_AXES[s]
        arrived, z_pending[s] = z_pending[s], []
        for copy, d, part in zip(arrived, (1, -1), halves):
            copy.wait_recv()
            origin = on(second, moved(me, second, -d)[second])
            ref = z_all.at[at((), me, **on(first, part), **origin) + (pl.ds(lo, hi - lo),)]
            z_pending[s].append(copies.start(ref, ref, chip(*moved(me, second, d))))

    vecs[...] = zeros(*vecs.shape)
    x_sums[...] = zeros(*x_sums.shape)
    got_x.wait()

    def element_tile(i, carry):
        rows = tile_rows(i, x_rows.shape[-1])
        d_v_low = dot(probs[rows, :], d_attn[...], NN).astype(BF16)
        d_k_low = dot(d_logits[rows, :], q[...], NN).astype(BF16)
        d_v[rows, :] = d_v_low
        d_k[rows, :] = d_k_low
        unit, rstd = norm_parts(x_rows[i], DOWN)
        x_norm[0:channels, rows] = (unit * x_gain[...] + x_shift[...]).astype(BF16)
        d_normed = (dot(w_key[...], d_k_low, NT) + dot(w_value[...], d_v_low, NT)).astype(BF16).astype(F32)
        d_x[i] = norm_pull(d_normed, unit, rstd, x_gain[...], DOWN)
        for h, value in enumerate((d_normed * unit, d_normed)):
            x_sums[h] += sum(value[:, t * LANES:(t + 1) * LANES] for t in range(value.shape[1] // LANES))
        return carry

    lax.fori_loop(0, SIDE, element_tile, 0)
    x_pending = []
    for d in HOPS:
        peer = moved(me, 0, d)
        x_pending.append(copies.start(d_x.at[peer[0]], d_x_in.at[z], chip(*peer)))
    d_x_in[z] = d_x[z]

    for s, (lo, hi) in enumerate(STREAM_ROWS):
        for copy in z_pending[s]:
            copy.wait_recv()

    def z_piece(s, i, place):
        first, second, third = STREAM_AXES[s]
        lo, hi = STREAM_ROWS[s]
        return z_all.at[at((second,), me, **on(first, i), **on(third, place)) + (pl.ds(lo, hi - lo),)]

    ring = {}

    def start_ring(step):
        for s in range(n):
            third = STREAM_AXES[s][2]
            right, left = moved(me, third, 1), moved(me, third, -1)
            place = me[third]
            for way, peer, i in (('right', right, step), ('left', left, SIDE - 1 - step)):
                ref = z_piece(s, i, place)
                ring[s, way, step] = copies.start(ref, ref, chip(*peer))

    forwarded = []

    def forward_ring(step):
        for s in range(n):
            third = STREAM_AXES[s][2]
            right, left = moved(me, third, 1), moved(me, third, -1)
            for way, peer, origin, i in (('right', right, left, step), ('left', left, right, SIDE - 1 - step)):
                ring.pop((s, way, step)).wait_recv()
                ref = z_piece(s, i, origin[third])
                forwarded.append(copies.start(ref, ref, chip(*peer)))

    start_ring(0)
    start_ring(1)

    for h in range(2):
        vecs[6 + h:7 + h, 0:channels] = total(x_sums[h].T)
    got_latents.wait()

    def latent_tile(i, carry):
        rows = tile_rows(i, LATENT_TILE)
        unit, rstd = norm_parts(latents[rows, :])
        z_norm[rows, :] = (unit * z_gain[...] + z_shift[...]).astype(BF16)
        d_normed = dot(d_q[rows, :], w_query[...], NT)
        for h, value in enumerate((d_normed * unit, d_normed)):
            vecs[4 + h:5 + h, :] += total(value)
        d_lat = norm_pull(d_normed, unit, rstd, z_gain[...])
        slab, part = lax.div(i, 2), lax.rem(i, 2)
        for t in range(split):
            block = d_lat[:, t * LANES:(t + 1) * LANES].reshape(2, SIDE, SIDE, 8, LANES)
            g[0, pl.ds(2 * part, 2), :, :, slab * split + t] = block
        return carry

    lax.fori_loop(0, tiles, latent_tile, 0)
    slab, part = y, x
    for t in range(split):
        g[0, part, :, :, slab * split + t] += d_mid[:, t * LANES:(t + 1) * LANES].reshape(SIDE, SIDE, 8, LANES)

    def put(value, start):
        for t in range(value.shape[1] // LANES):
            half, slot = tile_place(start + t)
            g[half, :, :, :, slot] = value[:, t * LANES:(t + 1) * LANES].reshape(SIDE, SIDE, SIDE, 8, LANES)

    put(dot(z_norm[...], d_q[...], TN), 4 * split)
    put(dot(x_norm[...], d_k[...], NN), 8 * split)
    put(dot(x_norm[...], d_v[...], NN), 9 * split)
    vecs[0:4, :] = vec_grads[0:4, :]
    half, slot = tile_place(8 * split)
    for i in range(vecs.shape[0]):
        for t in range(split):
            g[half, SIDE - 1, i // SIDE, i % SIDE, slot, t:t + 1, :] = vecs[i:i + 1, t * LANES:(t + 1) * LANES]
    for copy in got_w:
        copy.wait()

    core_half = copies.start(g.at[1 - dp], core_in, partner)
    core_half.wait_recv()
    for i in range(SIDE):
        for j in range(SIDE):
            g[dp, i, j] += core_in[i, j]
    copies.sent(core_half)
    pl.semaphore_signal(half_free, inc=1, device_id=partner, device_id_type=MESH_ID)

    def along(s, place, part=None):
        axis = STREAM_AXES[s][0]
        others = tuple(a for a in range(3) if a != axis)
        index = at(others, me, **on(axis, place), **({} if part is None else on(others[0], part)))
        lo, hi = STREAM_TILES[s]
        return (dp,) + index + (slice(lo, hi),)

    def send(index, dst_index, dst, peer):
        return copies.start(g.at[index], g.at[dst_index] if dst is None else dst, chip(*peer))

    ways = (1, -1)
    first = []
    for s in range(n):
        axis = STREAM_AXES[s][0]
        far = moved(me, axis, 2)[axis]
        first.append([send(along(s, far, halves[w]), None, side_in[s][w], moved(me, axis, d)) for w, d in enumerate(ways)])
    start_ring(2)
    pending = []
    for s in range(n):
        axis = STREAM_AXES[s][0]
        started = []
        for w, d in enumerate(ways):
            peer = moved(me, axis, d)
            first[s][w].wait_recv()
            g[along(s, peer[axis], halves[w])] += side_in[s][w][...]
            started.append(send(along(s, peer[axis]), None, full_in[s][w], peer))
        pending.append(started)
    for phase in range(1, 3):
        for s in range(n):
            for copy in pending[s]:
                copy.wait_recv()
            before, axis = STREAM_AXES[s][phase - 1], STREAM_AXES[s][phase]
            part = parts[s][phase - 1]
            left = [a for a in range(3) if a not in STREAM_AXES[s][:phase]]
            if phase == 1:
                for copy in first[s] + pending[s]:
                    copies.sent(copy)
                for i in range(SIDE):
                    part[i] = g[along(s, me[before], i)] + full_in[s][0][i] + full_in[s][1][i]
            else:
                for i in range(SIDE):
                    index = (me[before], i) if before < left[0] else (i, me[before])
                    part[i] = parts[s][0][index] + sum_slots(recvs[s][1], i)
            started = []
            for d in HOPS:
                peer = moved(me, axis, d)
                index = tuple(peer[axis] if a == axis else slice(None) for a in left)
                started.append(copies.start(part.at[index], recvs[s][phase].at[d - 1], chip(*peer)))
            pending[s] = started
        if phase == 1:
            start_ring(3)
        else:
            forward_ring(0)
    for s, (lo, hi) in enumerate(STREAM_TILES):
        for copy in pending[s]:
            copy.wait_recv()
        got, part = recvs[s][2], parts[s][1]
        axis = STREAM_AXES[s][2]
        g[(dp,) + me + (slice(lo, hi),)] = part[me[axis]] + sum_slots(got)
        ref = g.at[(dp,) + me + (pl.ds(lo, hi - lo),)]
        pending[s] = [copies.start(ref, ref, chip(*moved(me, axis, d))) for d in HOPS]
    forward_ring(1)
    core_copies = []
    pl.semaphore_wait(half_free, 1)
    for s, (lo, hi) in enumerate(STREAM_TILES):
        for copy in pending[s]:
            copy.wait_recv()
        _, axis, last = STREAM_AXES[s]
        ref = g.at[(dp,) + at((last,), me) + (pl.ds(lo, hi - lo),)]
        pending[s] = [copies.start(ref, ref, chip(*moved(me, axis, d))) for d in HOPS]

    def to_partner(index):
        core_copies.append(copies.start(g.at[index], g.at[index], partner))

    for s in range(n):
        for copy in pending[s]:
            copy.wait_recv()
        axis = STREAM_AXES[s][0]
        index = along(s, me[axis])
        pending[s] = [send(index, index, None, moved(me, axis, d)) for d in ways]
        to_partner(index)
    for copy in x_pending:
        copy.wait_recv()
    for i in range(SIDE):
        d_inputs[i] = d_x_in[i].astype(BF16)
    last = []
    for s in range(n):
        axis = STREAM_AXES[s][0]
        for w, d in enumerate(ways):
            pending[s][w].wait_recv()
            index = along(s, moved(me, axis, -d)[axis], halves[w])
            last.append((send(index, index, None, moved(me, axis, d)), s, w))
            to_partner(along(s, moved(me, axis, -d)[axis]))
    for copy, s, w in last:
        copy.wait_recv()
        axis = STREAM_AXES[s][0]
        to_partner(along(s, moved(me, axis, 2)[axis], halves[w]))
    for copy in core_copies:
        copy.wait_recv()

    outs = []
    for t in range(16):
        outs.append(fetch(g.at[0, :, :, :, t], d_lat_out.at[t // split, :, :, :, :, lanes(t % split)]))
    for t in range(16):
        half, slot = tile_place(16 + t)
        outs.append(fetch(g.at[half, :, :, :, slot], w_out_grads.at[t // split, :, :, :, :, lanes(t % split)]))
    for t in range(2 * split):
        half, slot = tile_place(8 * split + t)
        outs.append(fetch(g.at[half, :, :, :, slot], kv_out.at[t // split, :, :, :, :, lanes(t % split)]))
    half, slot = tile_place(8 * split)
    outs.append(fetch(g.at[half, SIDE - 1, :, :, slot], vec_out))
    for copy in forwarded + list(ring.values()):
        copy.wait_recv()
    copies.finish()
    for copy in outs:
        copy.wait()


def backward_block(q, k, v, d_attn, stats, top, z_rows, *others, collective_id):
    n_latents, width = q.shape
    x_rows, latents = others[-2:]
    elements, channels = k.shape[0], x_rows.shape[1]
    vmem = pl.BlockSpec(memory_space=pltpu.VMEM)
    hbm = pl.BlockSpec(memory_space=pl.ANY)
    cube, square = (SIDE, SIDE, SIDE), (SIDE, SIDE)
    shape, wide = jax.ShapeDtypeStruct, pltpu.VMEM
    block = x_rows.shape
    scratch = [
        wide((elements, n_latents), BF16), wide((elements, n_latents), BF16),
        wide((n_latents, width), BF16), wide((elements, width), BF16), wide((elements, width), BF16),
        wide(block, F32), wide((width, elements), BF16), wide((2, channels, LANES), F32), wide(block, F32), wide(block, F32),
        wide((n_latents, width), F32), wide((n_latents, width), BF16), wide((8, width), F32),
        wide((2,) + cube + (HALF_TILES, 8, LANES), F32), wide(cube + (HALF_TILES, 8, LANES), F32)]
    for lo, hi in STREAM_TILES:
        tiles = (hi - lo, 8, LANES)
        scratch += [wide((lead + tiles), F32) for lead in (
            (SIDE // 2, SIDE), (SIDE // 2, SIDE), square, square, (3, SIDE), (3,), square, (SIDE,))]
    n_copies = 160
    slab = cube + (8, width)
    return pl.pallas_call(
        backward_kernel,
        out_shape=(shape(cube + z_rows.shape, F32), shape(block, BF16), shape((4,) + slab, F32), shape((4,) + slab, F32),
                   shape((2,) + slab, F32), shape(square + (8, LANES), F32)),
        in_specs=[vmem] * 6 + [hbm] + [vmem] * (len(others) - 3) + [hbm] * 3,
        out_specs=(hbm, vmem, hbm, hbm, hbm, hbm),
        scratch_shapes=scratch + [pltpu.SemaphoreType.DMA((n_copies,)), pltpu.SemaphoreType.DMA((n_copies,)),
                                  pltpu.SemaphoreType.DMA((64,)), pltpu.SemaphoreType.REGULAR],
        compiler_params=pltpu.CompilerParams(
            collective_id=collective_id, has_side_effects=True, vmem_limit_bytes=VMEM_LIMIT),
    )(q, k, v, d_attn, stats, top, z_rows, *others)


def solution(mesh):
    x_spec = P('dp', 'cp', None)
    row_spec = P('dp', None, None)
    vec_spec = P(None)
    mat_spec = P(None, None)
    in_specs = (x_spec, mat_spec, vec_spec, vec_spec, vec_spec, vec_spec, mat_spec, mat_spec, mat_spec, mat_spec,
                vec_spec, vec_spec, mat_spec, vec_spec, mat_spec, vec_spec, row_spec)
    out_specs = (row_spec, x_spec, mat_spec, vec_spec, vec_spec, vec_spec, vec_spec, mat_spec, mat_spec, mat_spec, mat_spec,
                 vec_spec, vec_spec, mat_spec, vec_spec, mat_spec, vec_spec)

    def local_step(inputs, latents, x_gain, x_shift, z_gain, z_shift, w_query, w_key, w_value, w_out, m_gain, m_shift, w_up, b_up, w_down, b_down, d_out):
        batch, elements, channels = inputs.shape
        n_latents, width = latents.shape
        chunk = n_latents // PLANE
        z, y, x = chip_coords()
        owner = y * SIDE + x

        x_blocks = inputs.transpose(0, 2, 1).astype(F32)
        z0_rows = lax.dynamic_slice(latents, (owner * chunk, 0), (chunk, width))
        d_out_rows = lax.dynamic_slice(d_out, (z, owner * chunk, 0), (1, chunk, width))[0]
        row, column = (lambda vec: vec.reshape(1, -1)), (lambda vec: vec.reshape(-1, 1))
        norms = (column(x_gain), column(x_shift), row(z_gain), row(z_shift), w_query, w_key, w_value)
        q, k, v, x_in, z_out_rows, d_attn, stats, top, d_mid, w_grads, vec_grads = forward_block(
            x_blocks, latents, *norms, z0_rows, d_out_rows, w_out, w_up, w_down, row(m_gain), row(m_shift), row(b_up), row(b_down),
            collective_id=0)
        z_all, d_inputs, d_lat, w_sums, kv_sums, vec_sums = backward_block(
            q, k, v, d_attn.reshape(n_latents, width), stats, top, z_out_rows, d_mid, vec_grads, *norms,
            w_grads.reshape(3, SIDE, SIDE, SIDE, 8, width), x_in, latents, collective_id=1)
        w_sums = w_sums.reshape(4, width, width)
        kv_sums = kv_sums.reshape(2, width, width)[:, :channels]
        vec_sums = vec_sums[:2, :, :width // LANES].reshape(2 * SIDE, width)
        return (z_all.reshape(batch, n_latents, width), d_inputs.transpose(0, 2, 1), d_lat.reshape(n_latents, width),
                vec_sums[6, :channels], vec_sums[7, :channels], vec_sums[4], vec_sums[5],
                w_sums[0], kv_sums[0], kv_sums[1], w_sums[1], vec_sums[0], vec_sums[1],
                w_sums[2], vec_sums[2], w_sums[3], vec_sums[3])

    return jax.shard_map(local_step, mesh=mesh, in_specs=in_specs, out_specs=out_specs, check_vma=False)
```

time: 1500 us -> 290 us (0.19)
  blocking collectives: 1100 us -> 0 us
  Pallas kernels: 0 us -> 256 us
  matrix products: 180 us -> 0 us
  other arithmetic: 91.9 us -> 2.25 us
  waiting for transfers between devices: 52.2 us -> 0 us
  local copies, waits for them, and re-layouts: 51.4 us -> 31.1 us
    psum x4 -> x0, blocking collectives: 805 us -> none  [the longest x1 289 us: local_step(): lax.psum((jnp.sum(weights, axis=-1, keepdims=True), contract('bnm,bmv->bn...]
    pmax x1 -> x0, blocking collectives: 296 us -> none  [local_step(): row_max = lax.pmax(jnp.max(logits, axis=-1, keepdims=True), 'cp')]
    pallas_call x0 -> x2, Pallas kernels: none -> 256 us  [the longest x1 145 us: backward_block(): pl.pallas_call(backward_kernel, out_shape=(shape(cube + z_rows.shape, F32...]
    dot_general x24 -> x0, matrix products: 180 us -> none  [contract(): jnp.einsum(einsum_form, lhs_arr, rhs_arr, preferred_element_type=ACC_TYPE)]
    reduce_sum x11 -> x0, other arithmetic: 63.9 us -> none  [the longest x3 29.3 us: layer_norm(): return centred * lax.rsqrt(variance + LN_EPS) * ln_gain + ln_shift]
    psum x3 -> x0, waiting for transfers between devices: 52.1 us -> none  [the longest x1 31.3 us: local_step(): lax.psum(mlp_grads, 'dp')]
    unnamed x134 -> x6, local copies, waits for them, and re-layouts: 46 us -> 16.1 us
    convert_element_type x5 -> x1, other arithmetic: 21.7 us -> 2.25 us  [local_step(): x_blocks = inputs.transpose(0, 2, 1).astype(F32)]
  transfers between devices with their start and end apart: 3 -> 0, of which waited for: 2 -> 0; matrix products, arithmetic and copies ran while one was open for 6% -> 0% of each run, Pallas kernels for 0% -> 0%
where the time goes in v1:
time: 290 us
  Pallas kernels  256 us (88%)
  local copies, waits for them, and re-layouts  31.1 us (11%)
    pallas_call x1, Pallas kernels, backward_block(): pl.pallas_call(backward_kernel, out_shape=(shape(cube + z_rows.shape, F32...  145 us
    pallas_call x1, Pallas kernels, forward_block(): pl.pallas_call(forward_kernel, out_shape=(shape((latents_n, width), BF16)...  111 us
    unnamed x6, local copies, waits for them, and re-layouts  16.1 us

profile of v1, /device:TPU:1, one launch (start us, length us, event | category | flops | bytes accessed | tf_op | source)
XLA Modules:
  0.0 290.0 jit_solution(12253431328538784936)
XLA Ops:
  0.7 1.6 dynamic-slice_bitcast_fusion.d_out
  2.3 1.5 reshape.99.x_gain
  3.7 1.5 reshape.100.x_shift
  5.2 1.7 constant_dynamic-slice_fusion.z0
  6.8 2.3 convert_bitcast_fusion.x_blocks
  9.1 110.9 %shard_map.296 = (bf16[2048,512]{1,0:T(8,128)(2,1)}, bf16[1024,512]{1,0:T(8,128)(2,1)}, bf16[1024,512]{1,0:T(8,128)(2,1)}, f32[4,322,256]{2,1,0:T(8,128)}, f32[1...) custom-call(f32[4,322,256]{2,1,0:T(8,128)} %convert_bitcast_fusion.x, ...), custom_call_target="tpu_custom_call" | custom-call | tf_op jit(solution)/shard_map/pallas_call | solution.py:320
  120.0 145.0 %shard_map.297 = (f32[4,4,4,128,512]{4,3,2,1,0:T(8,128)}, bf16[4,322,256]{2,1,0:T(8,128)(2,1)}, f32[4,4,4,4,8,512]{5,4,3,2,1,0:T(8,128)}, f32[4,4,4,4,8,512]{5,4...) custom-call(bf16[2048,512]{1,0:T(8,128)(2,1)} %get-tuple-element.34.q, ...), custom_call_target="tpu_custom_call" | custom-call | tf_op jit(solution)/shard_map/pallas_call | solution.py:686
  265.0 2.2 copy.41
  267.1 0.8 slice.52
  267.9 0.6 slice_reduce_fusion
  268.5 0.6 fusion.1
  269.1 2.5 slice_bitcast_fusion
  271.6 4.5 %fusion = (f32[1,4,4,4,8,512]{5,4,3,2,1,0:T(8,128)}, f32[1,4,4,4,8,512]{5,4,3,2,1,0:T(8,128)}, f32[1,4,4,4,8,512]{5,4,3,2,1,0:T(8,128)}, f32[1,4,4,4,8,512]{5,4,3,2,1,0:T(8,128)}) fusion(f32[4,4,4,4,8,512]{5,4,3,2,1,0:T(8,128)} %get-tuple-element.49), kind=kLoop, calls=%fused_computation.8 | loop fusion | bytes 8388608 | tf_op jit(solution)/shard_map/slice | solution.py:733
  276.0 0.0 copy-start
  276.0 11.9 %copy.48 = f32[4,2048,512]{2,1,0:T(8,128)} copy(f32[4,2048,512]{2,1,0:T(8,128)} %bitcast.35) | data formatting | bytes 33554432
  287.9 0.0 copy-done
  287.9 2.0 copy.49
  (1 shorter events, 0.0 us)
Async XLA Ops:
  276.0 11.9 %copy-start = (f32[4,4,4,4,8,512]{5,4,3,2,1,0:T(8,128)S(1)}, f32[4,4,4,4,8,512]{5,4,3,2,1,0:T(8,128)}, u32[]{:S(2)}) copy-start(f32[4,4,4,4,8,512]{5,4,3,2,1,0:T(8,128)} %get-tuple-element.47) | copy-start | bytes 12582916

commit v2 on v1

--- a/solution.py
+++ b/solution.py
@@ -72,6 +72,10 @@
     return rstd * (d_unit - mean(d_unit, axis) - unit * mean(d_unit * unit, axis))
 
 
+def as_column(row):
+    return jnp.broadcast_to(row[...], (LANES, row.shape[1])).T[:, :1]
+
+
 def row_pair(ref, i):
     return jnp.concatenate([ref[pl.ds(2 * i, 1), :], ref[pl.ds(2 * i + 1, 1), :]], axis=ACROSS)
 
@@ -130,13 +134,39 @@
             copy.wait_send()
 
 
+class LocalCopies:
+    def __init__(self, sems):
+        self.sems, self.used = sems, 0
+
+    def start(self, src, dst):
+        copy = pltpu.make_async_copy(src, dst, self.sems.at[self.used])
+        self.used += 1
+        copy.start()
+        return copy
+
+
+def at(free, coords, **other):
+    index = []
+    for axis, name in enumerate('zyx'):
+        index.append(other[name] if name in other else (slice(None) if axis in free else coords[axis]))
+    return tuple(index)
+
+
+def on(axis, value):
+    return {'zyx'[axis]: value}
+
+
 def forward_kernel(
-        x_blocks, latents, x_gain, x_shift, z_gain, z_shift, w_query, w_key, w_value,
-        z0, d_out, w_out, w_up, w_down, m_gain, m_shift, b_up, b_down,
-        q, k, v, x_in, z_out, d_attn_all, stats_all, top_all, d_mid_out, w_grads, vec_grads,
-        vt, logits, mixed, top_own, tops, sum_own, sum_parts, sums, ra1, rb1, pa1, pb1, ra2, rb2, d_attn_f32, stats_f32,
-        send_sems, recv_sems):
+        x_blocks, latents_in, d_out_in, x_gain_row, x_shift_row, z_gain, z_shift, w_query, w_key, w_value,
+        w_out, w_up, w_down, m_gain, m_shift, b_up, b_down,
+        q_out, k_out, v_out, x_out, z_all, w_grads_out, d_attn_all, stats_all, top_all, d_mid_out, vec_grads,
+        q, k, v, x_in, latents, d_out, z_out, w_grads,
+        vt, logits, mixed, top_own, tops, sum_own, sum_parts, sums, sa, sb, fa, fb, pa1, pb1, ra2, rb2, d_attn_f32, stats_f32,
+        send_sems, recv_sems, local_sems):
     me = chip_coords()
+    local = LocalCopies(local_sems)
+    got_latents = local.start(latents_in, latents)
+    got_own = local.start(x_blocks.at[me[0]], x_in.at[me[0]])
     z, y, x = me
     owner = y * SIDE + x
     plane_peers = []
@@ -145,9 +175,13 @@
         plane_peers.append((other, chip(z, lax.div(other, SIDE), lax.rem(other, SIDE))))
     enter([device for _, device in plane_peers] + [chip(*moved(me, 0, d)) for d in HOPS])
     copies = Copies(send_sems, recv_sems)
+    chunk = d_out.shape[0]
+    got_d_out = local.start(d_out_in.at[z, pl.ds(owner * chunk, chunk), :], d_out)
     qk_scale = q.shape[1] ** -0.5
     to_log2 = qk_scale * LOG2E
     tiles = q.shape[0] // LATENT_TILE
+    halves = (slice(0, SIDE // 2), slice(SIDE // 2, SIDE))
+    ways = (1, -1)
     half_v = vt.shape[0] // 2
     block_rows = x_blocks.shape[-1]
 
@@ -155,8 +189,9 @@
     for d in HOPS:
         peer = moved(me, 0, d)
         got_x[d] = copies.start(x_blocks.at[peer[0]], x_in.at[z], chip(*peer))
-    x_in[z] = x_blocks[z]
     top_own[...] = jnp.full(top_own.shape, -jnp.inf, F32)
+    x_gain, x_shift = as_column(x_gain_row), as_column(x_shift_row)
+    got_latents.wait()
 
     def query_tile(i, carry):
         rows = tile_rows(i, LATENT_TILE)
@@ -166,11 +201,13 @@
         return carry
 
     lax.fori_loop(0, tiles, query_tile, 0)
+    saved = [local.start(q, q_out)]
+    got_own.wait()
 
     def block_logits(j):
         rows = tile_rows(j, block_rows)
         unit, _ = norm_parts(x_in[j], DOWN)
-        x_norm = (unit * x_gain[...] + x_shift[...]).astype(BF16)
+        x_norm = (unit * x_gain + x_shift).astype(BF16)
         k[rows, :] = dot(x_norm, w_key[...], TN).astype(BF16)
         v[rows, :] = dot(x_norm, w_value[...], TN).astype(BF16)
         vt[:, rows] = dot(w_value[...], x_norm, TN).astype(BF16)
@@ -191,6 +228,7 @@
         got_x[d].wait_recv()
         block_logits(moved(me, 0, -d)[0])
     top_own[...] = jnp.ceil(top_own[...] * to_log2)
+    saved += [local.start(k, k_out), local.start(v, v_out), local.start(x_in, x_out)]
     tops[owner] = top_own[...]
     top_copies = [copies.start(top_own, tops.at[owner], device) for _, device in plane_peers]
 
@@ -217,33 +255,40 @@
         mixed[i // SIDE, i % SIDE] = mixed[i // SIDE, i % SIDE] * factor[i:i + 1, :]
         sum_parts[i] = jnp.broadcast_to(scaled_sum[i:i + 1, :], (8, LANES))
 
-    first = [[], []]
-    for d in HOPS:
-        peer = moved(me, 2, d)
-        first[0].append(copies.start(mixed.at[:, peer[2], 0:half_v, :], ra1.at[d - 1], chip(*peer)))
-        peer = moved(me, 1, d)
-        first[1].append(copies.start(mixed.at[peer[1], :, half_v:2 * half_v, :], rb1.at[d - 1], chip(*peer)))
+    streams = ((2, 1, pl.ds(0, half_v), sa, fa, pa1, ra2), (1, 2, pl.ds(half_v, half_v), sb, fb, pb1, rb2))
+
+    def mixed_at(axis, place, part, cols):
+        return ((part, place) if axis == 2 else (place, part)) + (cols,)
+
+    first = []
+    for axis, _, cols, side_in, _, _, _ in streams:
+        far = moved(me, axis, 2)[axis]
+        first.append([copies.start(mixed.at[mixed_at(axis, far, halves[w], cols)], side_in.at[w], chip(*moved(me, axis, d)))
+                      for w, d in enumerate(ways)])
     sums[owner] = sum_parts[owner]
     sum_copies = [copies.start(sum_parts.at[other], sums.at[owner], device) for other, device in plane_peers]
-    for copy in first[0]:
-        copy.wait_recv()
-    second = [[], []]
-    for i in range(SIDE):
-        pa1[i] = mixed[i, x, 0:half_v, :] + sum_slots(ra1, i)
-    for d in HOPS:
-        peer = moved(me, 1, d)
-        second[0].append(copies.start(pa1.at[peer[1]], ra2.at[d - 1], chip(*peer)))
-    for copy in first[1]:
-        copy.wait_recv()
-    for i in range(SIDE):
-        pb1[i] = mixed[y, i, half_v:2 * half_v, :] + sum_slots(rb1, i)
-    for d in HOPS:
-        peer = moved(me, 2, d)
-        second[1].append(copies.start(pb1.at[peer[2]], rb2.at[d - 1], chip(*peer)))
+    full = []
+    for (axis, _, cols, side_in, full_in, _, _), arriving in zip(streams, first):
+        started = []
+        for w, d in enumerate(ways):
+            peer = moved(me, axis, d)
+            arriving[w].wait_recv()
+            mixed[mixed_at(axis, peer[axis], halves[w], cols)] += side_in[w]
+            started.append(copies.start(mixed.at[mixed_at(axis, peer[axis], slice(None), cols)], full_in.at[w], chip(*peer)))
+        full.append(started)
+    second = []
+    for (axis, other, cols, _, full_in, part, slots), arriving in zip(streams, full):
+        for copy in arriving:
+            copy.wait_recv()
+        for i in range(SIDE):
+            part[i] = mixed[mixed_at(axis, me[axis], i, cols)] + full_in[0, i] + full_in[1, i]
+        for d in HOPS:
+            peer = moved(me, other, d)
+            second.append(copies.start(part.at[peer[other]], slots.at[d - 1], chip(*peer)))
     for copy in sum_copies:
         copy.wait_recv()
     inv_sum = 1.0 / functools.reduce(lambda a, b: a + b, [sums[i] for i in range(PLANE)])
-    for copy in second[0] + second[1]:
+    for copy in second:
         copy.wait_recv()
     upper = pa1[y] + sum_slots(ra2)
     lower = pb1[x] + sum_slots(rb2)
@@ -251,7 +296,7 @@
 
     attn_t_low = attn_t.astype(BF16)
     attn_low = attn_t.T.astype(BF16)
-    z_mid = z0[...] + dot(attn_low, w_out[...], NN)
+    z_mid = latents[tile_rows(owner, chunk), :] + dot(attn_low, w_out[...], NN)
     unit, rstd = norm_parts(z_mid)
     hidden_f32 = unit * m_gain[...] + m_shift[...]
     hidden = hidden_f32.astype(BF16)
@@ -260,6 +305,7 @@
     act = act_f32.astype(BF16)
     z_out[...] = z_mid + dot(act, w_down[...], NN) + b_down[...]
 
+    got_d_out.wait()
     d_out_low = d_out[...]
     d_out_f32 = d_out_low.astype(F32)
     d_act = dot(d_out_low, w_down[...], NT).astype(BF16).astype(F32)
@@ -282,72 +328,74 @@
         first[1].append(copies.start(d_attn_f32.at[y, x, down], d_attn_f32.at[y, x, down], chip(*moved(me, 2, d))))
     stat_copies = [copies.start(stats_f32.at[owner], stats_f32.at[owner], device) for _, device in plane_peers]
 
+    saved.append(local.start(z_out, z_all.at[z, y, x]))
+    z_first = []
+    for (lo, hi), (axis, _, _) in zip(STREAM_ROWS, STREAM_AXES):
+        rows = pl.ds(lo, hi - lo)
+        z_first += [copies.start(z_out.at[rows], z_all.at[z, y, x, rows], chip(*moved(me, axis, d))) for d in HOPS]
+
     d_mid_out[...] = d_mid
     w_grads[0] = dot(attn_t_low, d_mid_low, NN)
     w_grads[1] = dot(hidden_f32.T.astype(BF16), d_pre_low, NN)
     w_grads[2] = dot(act_f32.T.astype(BF16), d_out_low, NN)
+    saved.append(local.start(w_grads, w_grads_out))
     for i, value in enumerate((d_hidden * unit, d_hidden, d_pre, d_out_f32)):
         vec_grads[i:i + 1, :] = total(value)
     vec_grads[4:8, :] = zeros(4, vec_grads.shape[1])
 
-    second = []
-    for copy in first[0]:
-        copy.wait_recv()
-    for d in HOPS:
-        second.append(copies.start(d_attn_f32.at[:, x, up], d_attn_f32.at[:, x, up], chip(*moved(me, 2, d))))
-    for copy in first[1]:
-        copy.wait_recv()
-    for d in HOPS:
-        second.append(copies.start(d_attn_f32.at[y, :, down], d_attn_f32.at[y, :, down], chip(*moved(me, 1, d))))
-    for copy in stat_copies + second:
+    gathered = []
+    for axis, rows, arriving in ((2, up, first[0]), (1, down, first[1])):
+        for copy in arriving:
+            copy.wait_recv()
+        ref = d_attn_f32.at[mixed_at(axis, me[axis], slice(None), rows)]
+        gathered.append((axis, rows, [copies.start(ref, ref, chip(*moved(me, axis, d))) for d in ways]))
+    last = []
+    for axis, rows, arriving in gathered:
+        for w, d in enumerate(ways):
+            arriving[w].wait_recv()
+            ref = d_attn_f32.at[mixed_at(axis, moved(me, axis, -d)[axis], halves[w], rows)]
+            last.append(copies.start(ref, ref, chip(*moved(me, axis, d))))
+    for copy in stat_copies + last + z_first:
         copy.wait_recv()
     copies.finish()
     stats_all[...] = stats_f32[...]
     for i in range(PLANE):
         d_attn_all[i] = d_attn_f32[i // SIDE, i % SIDE].astype(BF16)
-
-
-def forward_block(x_blocks, latents, *others, collective_id):
+    for copy in saved:
+        copy.wait()
+
+
+def forward_block(x_blocks, latents, d_out, *others, collective_id):
     latents_n, width = latents.shape
     _, channels, block_rows = x_blocks.shape
     elements = SIDE * block_rows
     chunk = latents_n // PLANE
     half = width // 2
     vmem = pl.BlockSpec(memory_space=pltpu.VMEM)
-    n_copies = 3 * PLANE + 24
+    hbm = pl.BlockSpec(memory_space=pl.ANY)
+    n_copies = 90
     shape, wide = jax.ShapeDtypeStruct, pltpu.VMEM
-    stat, slots = (PLANE, 8, LANES), (3, SIDE, half, LANES)
+    stat, slots = (PLANE, 8, LANES), (2, SIDE, half, LANES)
+    saved = (((latents_n, width), BF16), ((elements, width), BF16), ((elements, width), BF16), (x_blocks.shape, F32))
     return pl.pallas_call(
         forward_kernel,
-        out_shape=(
-            shape((latents_n, width), BF16), shape((elements, width), BF16), shape((elements, width), BF16),
-            shape(x_blocks.shape, F32), shape((chunk, width), F32), shape((PLANE, chunk, width), BF16),
-            shape(stat, F32), shape((PLANE, LANES), F32), shape((chunk, width), F32), shape((3, width, width), F32),
-            shape((8, width), F32)),
-        in_specs=[vmem] * (2 + len(others)),
-        out_specs=(vmem,) * 11,
-        scratch_shapes=[
+        out_shape=tuple(shape(*one) for one in saved) + (
+            shape((SIDE, SIDE, SIDE, chunk, width), F32), shape((3, width, width), F32), shape((PLANE, chunk, width), BF16),
+            shape(stat, F32), shape((PLANE, LANES), F32), shape((chunk, width), F32), shape((8, width), F32)),
+        in_specs=[hbm] * 3 + [vmem] * len(others),
+        out_specs=(hbm,) * 6 + (vmem,) * 5,
+        scratch_shapes=[wide(*one) for one in saved] + [
+            wide((latents_n, width), F32), wide((chunk, width), BF16), wide((chunk, width), F32), wide((3, width, width), F32),
             wide((width, elements), BF16), wide((latents_n // LATENT_TILE, elements, LATENT_TILE), F32),
             wide((SIDE, SIDE, width, LANES), F32),
             wide((PLANE, LANES), F32), wide((PLANE, PLANE, LANES), F32), wide((PLANE, LANES), F32), wide(stat, F32), wide(stat, F32),
-            wide(slots, F32), wide(slots, F32), wide(slots[1:], F32), wide(slots[1:], F32),
-            wide((3, half, LANES), F32), wide((3, half, LANES), F32),
+            wide((2, SIDE // 2, half, LANES), F32), wide((2, SIDE // 2, half, LANES), F32), wide(slots, F32), wide(slots, F32),
+            wide(slots[1:], F32), wide(slots[1:], F32), wide((3, half, LANES), F32), wide((3, half, LANES), F32),
             wide((SIDE, SIDE, chunk, width), F32), wide(stat, F32),
-            pltpu.SemaphoreType.DMA((n_copies,)), pltpu.SemaphoreType.DMA((n_copies,))],
+            pltpu.SemaphoreType.DMA((n_copies,)), pltpu.SemaphoreType.DMA((n_copies,)), pltpu.SemaphoreType.DMA((16,))],
         compiler_params=pltpu.CompilerParams(
             collective_id=collective_id, has_side_effects=True, vmem_limit_bytes=VMEM_LIMIT),
-    )(x_blocks, latents, *others)
-
-
-def at(free, coords, **other):
-    index = []
-    for axis, name in enumerate('zyx'):
-        index.append(other[name] if name in other else (slice(None) if axis in free else coords[axis]))
-    return tuple(index)
-
-
-def on(axis, value):
-    return {'zyx'[axis]: value}
+    )(x_blocks, latents, d_out, *others)
 
 
 def tile_place(t):
@@ -355,10 +403,10 @@
 
 
 def backward_kernel(
-        q, k, v, d_attn, stats, top, z_rows, d_mid, vec_grads, x_gain, x_shift, z_gain, z_shift, w_query, w_key, w_value,
-        w_grads, x_in, latents_in,
+        q_in, k_in, v_in, d_attn_in, z_in, stats, top, d_mid, vec_grads, x_gain_row, x_shift_row, z_gain, z_shift,
+        w_query, w_key, w_value, w_grads, x_in, latents_in,
         z_all, d_inputs, d_lat_out, w_out_grads, kv_out, vec_out,
-        probs, d_logits, d_q, d_k, d_v, x_rows, x_norm, x_sums, d_x, d_x_in, latents, z_norm, vecs, g, core_in, *rest):
+        q, k, v, d_attn, probs, d_logits, d_q, d_k, d_v, x_rows, x_norm, x_sums, d_x, d_x_in, latents, z_norm, vecs, g, core_in, *rest):
     n, per = len(STREAM_TILES), 8
     side_in = [rest[per * s:per * s + 2] for s in range(n)]
     full_in = [rest[per * s + 2:per * s + 4] for s in range(n)]
@@ -378,23 +426,17 @@
     split = width // LANES
     chips = SIDE ** 3
 
-    local = []
-
-    def fetch(src, dst):
-        copy = pltpu.make_async_copy(src, dst, local_sems.at[len(local)])
-        copy.start()
-        local.append(copy)
-        return copy
-
+    local = LocalCopies(local_sems)
+    fetch = local.start
+    got_first = [fetch(*pair) for pair in ((q_in, q), (k_in, k), (v_in, v), (d_attn_in, d_attn))]
     enter([partner] + [chip(*moved(me, axis, d)) for axis in range(3) for d in HOPS])
     copies = Copies(send_sems, recv_sems)
 
-    own_z = fetch(z_rows, z_all.at[z, y, x])
+    ways = (1, -1)
     z_pending = []
-    for s, (lo, hi) in enumerate(STREAM_ROWS):
-        rows = pl.ds(lo, hi - lo)
-        z_pending.append([
-            copies.start(z_rows.at[rows], z_all.at[z, y, x, rows], chip(*moved(me, STREAM_AXES[s][0], d))) for d in HOPS])
+    for (lo, hi), (first, second, _) in zip(STREAM_ROWS, STREAM_AXES):
+        ref = z_all.at[at((first,), me) + (pl.ds(lo, hi - lo),)]
+        z_pending.append([copies.start(ref, ref, chip(*moved(me, second, d))) for d in ways])
     got_x = fetch(x_in, x_rows)
     got_latents = fetch(latents_in, latents)
     got_w = []
@@ -403,6 +445,9 @@
             half, slot = tile_place(20 + split * i + t)
             got_w.append(fetch(w_grads.at[i, :, :, :, :, lanes(t)], g.at[half, :, :, :, slot]))
     x_norm[...] = jnp.zeros(x_norm.shape, BF16)
+    x_gain, x_shift = as_column(x_gain_row), as_column(x_shift_row)
+    for copy in got_first:
+        copy.wait()
 
     def pair(ref, i, row):
         return jnp.concatenate([ref[2 * i + h, row:row + 1, :] for h in range(2)], axis=ACROSS)
@@ -420,48 +465,16 @@
         return carry
 
     lax.fori_loop(0, tiles // 2, attend_tile, 0)
-    own_z.wait()
-    for s, (lo, hi) in enumerate(STREAM_ROWS):
-        for copy in z_pending[s]:
-            copy.wait_recv()
-        first, second, _ = STREAM_AXES[s]
-        ref = z_all.at[at((first,), me) + (pl.ds(lo, hi - lo),)]
-        z_pending[s] = [copies.start(ref, ref, chip(*moved(me, second, d))) for d in (1, -1)]
-    lax.fori_loop(tiles // 2, tiles, attend_tile, 0)
-
     for s, (lo, hi) in enumerate(STREAM_ROWS):
         first, second, _ = STREAM_AXES[s]
         arrived, z_pending[s] = z_pending[s], []
-        for copy, d, part in zip(arrived, (1, -1), halves):
+        for copy, d, part in zip(arrived, ways, halves):
             copy.wait_recv()
             origin = on(second, moved(me, second, -d)[second])
             ref = z_all.at[at((), me, **on(first, part), **origin) + (pl.ds(lo, hi - lo),)]
             z_pending[s].append(copies.start(ref, ref, chip(*moved(me, second, d))))
 
-    vecs[...] = zeros(*vecs.shape)
-    x_sums[...] = zeros(*x_sums.shape)
-    got_x.wait()
-
-    def element_tile(i, carry):
-        rows = tile_rows(i, x_rows.shape[-1])
-        d_v_low = dot(probs[rows, :], d_attn[...], NN).astype(BF16)
-        d_k_low = dot(d_logits[rows, :], q[...], NN).astype(BF16)
-        d_v[rows, :] = d_v_low
-        d_k[rows, :] = d_k_low
-        unit, rstd = norm_parts(x_rows[i], DOWN)
-        x_norm[0:channels, rows] = (unit * x_gain[...] + x_shift[...]).astype(BF16)
-        d_normed = (dot(w_key[...], d_k_low, NT) + dot(w_value[...], d_v_low, NT)).astype(BF16).astype(F32)
-        d_x[i] = norm_pull(d_normed, unit, rstd, x_gain[...], DOWN)
-        for h, value in enumerate((d_normed * unit, d_normed)):
-            x_sums[h] += sum(value[:, t * LANES:(t + 1) * LANES] for t in range(value.shape[1] // LANES))
-        return carry
-
-    lax.fori_loop(0, SIDE, element_tile, 0)
-    x_pending = []
-    for d in HOPS:
-        peer = moved(me, 0, d)
-        x_pending.append(copies.start(d_x.at[peer[0]], d_x_in.at[z], chip(*peer)))
-    d_x_in[z] = d_x[z]
+    lax.fori_loop(tiles // 2, tiles, attend_tile, 0)
 
     for s, (lo, hi) in enumerate(STREAM_ROWS):
         for copy in z_pending[s]:
@@ -496,6 +509,31 @@
 
     start_ring(0)
     start_ring(1)
+
+    vecs[...] = zeros(*vecs.shape)
+    x_sums[...] = zeros(*x_sums.shape)
+    got_x.wait()
+
+    def element_tile(i, carry):
+        rows = tile_rows(i, x_rows.shape[-1])
+        d_v_low = dot(probs[rows, :], d_attn[...], NN).astype(BF16)
+        d_k_low = dot(d_logits[rows, :], q[...], NN).astype(BF16)
+        d_v[rows, :] = d_v_low
+        d_k[rows, :] = d_k_low
+        unit, rstd = norm_parts(x_rows[i], DOWN)
+        x_norm[0:channels, rows] = (unit * x_gain + x_shift).astype(BF16)
+        d_normed = (dot(w_key[...], d_k_low, NT) + dot(w_value[...], d_v_low, NT)).astype(BF16).astype(F32)
+        d_x[i] = norm_pull(d_normed, unit, rstd, x_gain, DOWN)
+        for h, value in enumerate((d_normed * unit, d_normed)):
+            x_sums[h] += sum(value[:, t * LANES:(t + 1) * LANES] for t in range(value.shape[1] // LANES))
+        return carry
+
+    lax.fori_loop(0, SIDE, element_tile, 0)
+    x_pending = []
+    for d in HOPS:
+        peer = moved(me, 0, d)
+        x_pending.append(copies.start(d_x.at[peer[0]], d_x_in.at[z], chip(*peer)))
+    d_x_in[z] = d_x[z]
 
     for h in range(2):
         vecs[6 + h:7 + h, 0:channels] = total(x_sums[h].T)
@@ -554,7 +592,6 @@
     def send(index, dst_index, dst, peer):
         return copies.start(g.at[index], g.at[dst_index] if dst is None else dst, chip(*peer))
 
-    ways = (1, -1)
     first = []
     for s in range(n):
         axis = STREAM_AXES[s][0]
@@ -662,7 +699,7 @@
         copy.wait()
 
 
-def backward_block(q, k, v, d_attn, stats, top, z_rows, *others, collective_id):
+def backward_block(q, k, v, d_attn, z_all, *others, collective_id):
     n_latents, width = q.shape
     x_rows, latents = others[-2:]
     elements, channels = k.shape[0], x_rows.shape[1]
@@ -672,7 +709,7 @@
     shape, wide = jax.ShapeDtypeStruct, pltpu.VMEM
     block = x_rows.shape
     scratch = [
-        wide((elements, n_latents), BF16), wide((elements, n_latents), BF16),
+        wide(q.shape, BF16), wide(k.shape, BF16), wide(v.shape, BF16), wide(q.shape, BF16), wide((elements, n_latents), BF16), wide((elements, n_latents), BF16),
         wide((n_latents, width), BF16), wide((elements, width), BF16), wide((elements, width), BF16),
         wide(block, F32), wide((width, elements), BF16), wide((2, channels, LANES), F32), wide(block, F32), wide(block, F32),
         wide((n_latents, width), F32), wide((n_latents, width), BF16), wide((8, width), F32),
@@ -685,15 +722,16 @@
     slab = cube + (8, width)
     return pl.pallas_call(
         backward_kernel,
-        out_shape=(shape(cube + z_rows.shape, F32), shape(block, BF16), shape((4,) + slab, F32), shape((4,) + slab, F32),
+        out_shape=(shape(z_all.shape, F32), shape(block, BF16), shape((4,) + slab, F32), shape((4,) + slab, F32),
                    shape((2,) + slab, F32), shape(square + (8, LANES), F32)),
-        in_specs=[vmem] * 6 + [hbm] + [vmem] * (len(others) - 3) + [hbm] * 3,
+        in_specs=[hbm] * 5 + [vmem] * (len(others) - 3) + [hbm] * 3,
         out_specs=(hbm, vmem, hbm, hbm, hbm, hbm),
+        input_output_aliases={4: 0},
         scratch_shapes=scratch + [pltpu.SemaphoreType.DMA((n_copies,)), pltpu.SemaphoreType.DMA((n_copies,)),
                                   pltpu.SemaphoreType.DMA((64,)), pltpu.SemaphoreType.REGULAR],
         compiler_params=pltpu.CompilerParams(
             collective_id=collective_id, has_side_effects=True, vmem_limit_bytes=VMEM_LIMIT),
-    )(q, k, v, d_attn, stats, top, z_rows, *others)
+    )(q, k, v, d_attn, z_all, *others)
 
 
 def solution(mesh):
@@ -714,15 +752,12 @@
         owner = y * SIDE + x
 
         x_blocks = inputs.transpose(0, 2, 1).astype(F32)
-        z0_rows = lax.dynamic_slice(latents, (owner * chunk, 0), (chunk, width))
-        d_out_rows = lax.dynamic_slice(d_out, (z, owner * chunk, 0), (1, chunk, width))[0]
-        row, column = (lambda vec: vec.reshape(1, -1)), (lambda vec: vec.reshape(-1, 1))
-        norms = (column(x_gain), column(x_shift), row(z_gain), row(z_shift), w_query, w_key, w_value)
-        q, k, v, x_in, z_out_rows, d_attn, stats, top, d_mid, w_grads, vec_grads = forward_block(
-            x_blocks, latents, *norms, z0_rows, d_out_rows, w_out, w_up, w_down, row(m_gain), row(m_shift), row(b_up), row(b_down),
-            collective_id=0)
+        row = lambda vec: vec.reshape(1, -1)
+        norms = (row(x_gain), row(x_shift), row(z_gain), row(z_shift), w_query, w_key, w_value)
+        q, k, v, x_in, z_all, w_grads, d_attn, stats, top, d_mid, vec_grads = forward_block(
+            x_blocks, latents, d_out, *norms, w_out, w_up, w_down, row(m_gain), row(m_shift), row(b_up), row(b_down), collective_id=0)
         z_all, d_inputs, d_lat, w_sums, kv_sums, vec_sums = backward_block(
-            q, k, v, d_attn.reshape(n_latents, width), stats, top, z_out_rows, d_mid, vec_grads, *norms,
+            q, k, v, d_attn.reshape(n_latents, width), z_all, stats, top, d_mid, vec_grads, *norms,
             w_grads.reshape(3, SIDE, SIDE, SIDE, 8, width), x_in, latents, collective_id=1)
         w_sums = w_sums.reshape(4, width, width)
         kv_sums = kv_sums.reshape(2, width, width)[:, :channels]

time: 290 us -> 271 us (0.934)
  Pallas kernels: 256 us -> 240 us
  local copies, waits for them, and re-layouts: 31.1 us -> 27.5 us
    pallas_call x2, Pallas kernels: 256 us -> 240 us  [the longest x1 147 us: backward_block(): pl.pallas_call(backward_kernel, out_shape=(shape(z_all.shape, F32), shape...]
where the time goes in v2:
time: 271 us; the launch traced here: 270 us
  Pallas kernels  240 us (89%)
  local copies, waits for them, and re-layouts  27.5 us (10%)
    pallas_call x1, Pallas kernels, backward_block(): pl.pallas_call(backward_kernel, out_shape=(shape(z_all.shape, F32), shape...  147 us
    pallas_call x1, Pallas kernels, forward_block(): pl.pallas_call(forward_kernel, out_shape=tuple((shape(*one) for one in sa...  93.2 us
    unnamed x6, local copies, waits for them, and re-layouts  16.1 us

profile of v2, /device:TPU:1, one launch (start us, length us, event | category | flops | bytes accessed | tf_op | source)
XLA Modules:
  0.0 270.3 jit_solution(17789213124283055602)
XLA Ops:
  0.7 1.2 reshape.85.x_gain_row
  1.9 1.2 reshape.86.x_shift_row
  3.1 2.3 convert_bitcast_fusion.x_blocks
  5.4 93.2 %shard_map.296 = (bf16[2048,512]{1,0:T(8,128)(2,1)}, bf16[1024,512]{1,0:T(8,128)(2,1)}, bf16[1024,512]{1,0:T(8,128)(2,1)}, f32[4,322,256]{2,1,0:T(8,128)}, f32[4...) custom-call(f32[4,322,256]{2,1,0:T(8,128)} %convert_bitcast_fusion.x, ...), custom_call_target="tpu_custom_call" | custom-call | tf_op jit(solution)/shard_map/pallas_call | solution.py:380
  98.6 146.7 %shard_map.297 = (f32[4,4,4,128,512]{4,3,2,1,0:T(8,128)}, bf16[4,322,256]{2,1,0:T(8,128)(2,1)}, f32[4,4,4,4,8,512]{5,4,3,2,1,0:T(8,128)}, f32[4,4,4,4,8,512]{5,4...) custom-call(bf16[2048,512]{1,0:T(8,128)(2,1)} %get-tuple-element.34., ...), custom_call_target="tpu_custom_call", output_to_operand_aliasing={{0}: (4, {})} | custom-call | tf_op jit(solution)/shard_map/pallas_call | solution.py:723
  245.3 2.2 copy.36
  247.5 0.8 slice.52
  248.3 0.6 slice_reduce_fusion
  248.9 0.6 fusion.1
  249.5 2.5 slice_bitcast_fusion
  251.9 4.5 %fusion = (f32[1,4,4,4,8,512]{5,4,3,2,1,0:T(8,128)}, f32[1,4,4,4,8,512]{5,4,3,2,1,0:T(8,128)}, f32[1,4,4,4,8,512]{5,4,3,2,1,0:T(8,128)}, f32[1,4,4,4,8,512]{5,4,3,2,1,0:T(8,128)}) fusion(f32[4,4,4,4,8,512]{5,4,3,2,1,0:T(8,128)} %get-tuple-element.49), kind=kLoop, calls=%fused_computation.6 | loop fusion | bytes 8388608 | tf_op jit(solution)/shard_map/slice | solution.py:768
  256.4 0.0 copy-start
  256.4 11.9 %copy.44 = f32[4,2048,512]{2,1,0:T(8,128)} copy(f32[4,2048,512]{2,1,0:T(8,128)} %bitcast.33) | data formatting | bytes 33554432
  268.3 0.0 copy-done
  268.3 2.0 copy.45
  (1 shorter events, 0.0 us)
Async XLA Ops:
  256.4 11.9 %copy-start = (f32[4,4,4,4,8,512]{5,4,3,2,1,0:T(8,128)S(1)}, f32[4,4,4,4,8,512]{5,4,3,2,1,0:T(8,128)}, u32[]{:S(2)}) copy-start(f32[4,4,4,4,8,512]{5,4,3,2,1,0:T(8,128)} %get-tuple-element.47) | copy-start | bytes 12582916

commit v3 on v2

--- a/solution.py
+++ b/solution.py
@@ -398,8 +398,12 @@
     )(x_blocks, latents, d_out, *others)
 
 
-def tile_place(t):
-    return t // HALF_TILES, t % HALF_TILES
+MLP_AT, LATENTS_AT, QUERY_AT, KEY_AT, VALUE_AT = 0, 3, 7, 8, 9
+SLOT_GROUPS = ((0, 6), (6, 14), (14, 20))
+
+
+def tile_place(matrix, t):
+    return t // 2, 2 * matrix + t % 2
 
 
 def backward_kernel(
@@ -442,7 +446,7 @@
     got_w = []
     for i in range(3):
         for t in range(split):
-            half, slot = tile_place(20 + split * i + t)
+            half, slot = tile_place(MLP_AT + i, t)
             got_w.append(fetch(w_grads.at[i, :, :, :, :, lanes(t)], g.at[half, :, :, :, slot]))
     x_norm[...] = jnp.zeros(x_norm.shape, BF16)
     x_gain, x_shift = as_column(x_gain_row), as_column(x_shift_row)
@@ -509,6 +513,17 @@
 
     start_ring(0)
     start_ring(1)
+
+    exchanged = []
+
+    def exchange(group):
+        lo, hi = SLOT_GROUPS[group]
+        slots = (slice(None),) * 3 + (pl.ds(lo, hi - lo),)
+        exchanged.append(copies.start(g.at[(1 - dp,) + slots], core_in.at[slots], partner))
+
+    for copy in got_w:
+        copy.wait()
+    exchange(0)
 
     vecs[...] = zeros(*vecs.shape)
     x_sums[...] = zeros(*x_sums.shape)
@@ -550,36 +565,41 @@
         slab, part = lax.div(i, 2), lax.rem(i, 2)
         for t in range(split):
             block = d_lat[:, t * LANES:(t + 1) * LANES].reshape(2, SIDE, SIDE, 8, LANES)
-            g[0, pl.ds(2 * part, 2), :, :, slab * split + t] = block
+            half, slot = tile_place(LATENTS_AT + slab, t)
+            g[half, pl.ds(2 * part, 2), :, :, slot] = block
         return carry
 
     lax.fori_loop(0, tiles, latent_tile, 0)
     slab, part = y, x
     for t in range(split):
-        g[0, part, :, :, slab * split + t] += d_mid[:, t * LANES:(t + 1) * LANES].reshape(SIDE, SIDE, 8, LANES)
-
-    def put(value, start):
-        for t in range(value.shape[1] // LANES):
-            half, slot = tile_place(start + t)
+        half, slot = tile_place(LATENTS_AT + slab, t)
+        g[half, part, :, :, slot] += d_mid[:, t * LANES:(t + 1) * LANES].reshape(SIDE, SIDE, 8, LANES)
+
+    exchange(1)
+
+    def put(value, matrix):
+        for t in range(split):
+            half, slot = tile_place(matrix, t)
             g[half, :, :, :, slot] = value[:, t * LANES:(t + 1) * LANES].reshape(SIDE, SIDE, SIDE, 8, LANES)
 
-    put(dot(z_norm[...], d_q[...], TN), 4 * split)
-    put(dot(x_norm[...], d_k[...], NN), 8 * split)
-    put(dot(x_norm[...], d_v[...], NN), 9 * split)
+    put(dot(z_norm[...], d_q[...], TN), QUERY_AT)
+    put(dot(x_norm[...], d_k[...], NN), KEY_AT)
+    put(dot(x_norm[...], d_v[...], NN), VALUE_AT)
     vecs[0:4, :] = vec_grads[0:4, :]
-    half, slot = tile_place(8 * split)
+    half, slot = tile_place(KEY_AT, 0)
     for i in range(vecs.shape[0]):
         for t in range(split):
             g[half, SIDE - 1, i // SIDE, i % SIDE, slot, t:t + 1, :] = vecs[i:i + 1, t * LANES:(t + 1) * LANES]
-    for copy in got_w:
-        copy.wait()
-
-    core_half = copies.start(g.at[1 - dp], core_in, partner)
-    core_half.wait_recv()
-    for i in range(SIDE):
-        for j in range(SIDE):
-            g[dp, i, j] += core_in[i, j]
-    copies.sent(core_half)
+    exchange(2)
+    start_ring(2)
+
+    for copy, (lo, hi) in zip(exchanged, SLOT_GROUPS):
+        copy.wait_recv()
+        for i in range(SIDE):
+            for j in range(SIDE):
+                g[dp, i, j, :, lo:hi] += core_in[i, j, :, lo:hi]
+    for copy in exchanged:
+        copies.sent(copy)
     pl.semaphore_signal(half_free, inc=1, device_id=partner, device_id_type=MESH_ID)
 
     def along(s, place, part=None):
@@ -597,7 +617,7 @@
         axis = STREAM_AXES[s][0]
         far = moved(me, axis, 2)[axis]
         first.append([send(along(s, far, halves[w]), None, side_in[s][w], moved(me, axis, d)) for w, d in enumerate(ways)])
-    start_ring(2)
+    start_ring(3)
     pending = []
     for s in range(n):
         axis = STREAM_AXES[s][0]
@@ -630,10 +650,7 @@
                 index = tuple(peer[axis] if a == axis else slice(None) for a in left)
                 started.append(copies.start(part.at[index], recvs[s][phase].at[d - 1], chip(*peer)))
             pending[s] = started
-        if phase == 1:
-            start_ring(3)
-        else:
-            forward_ring(0)
+        forward_ring(phase - 1)
     for s, (lo, hi) in enumerate(STREAM_TILES):
         for copy in pending[s]:
             copy.wait_recv()
@@ -642,7 +659,6 @@
         g[(dp,) + me + (slice(lo, hi),)] = part[me[axis]] + sum_slots(got)
         ref = g.at[(dp,) + me + (pl.ds(lo, hi - lo),)]
         pending[s] = [copies.start(ref, ref, chip(*moved(me, axis, d))) for d in HOPS]
-    forward_ring(1)
     core_copies = []
     pl.semaphore_wait(half_free, 1)
     for s, (lo, hi) in enumerate(STREAM_TILES):
@@ -682,15 +698,13 @@
         copy.wait_recv()
 
     outs = []
-    for t in range(16):
-        outs.append(fetch(g.at[0, :, :, :, t], d_lat_out.at[t // split, :, :, :, :, lanes(t % split)]))
-    for t in range(16):
-        half, slot = tile_place(16 + t)
-        outs.append(fetch(g.at[half, :, :, :, slot], w_out_grads.at[t // split, :, :, :, :, lanes(t % split)]))
-    for t in range(2 * split):
-        half, slot = tile_place(8 * split + t)
-        outs.append(fetch(g.at[half, :, :, :, slot], kv_out.at[t // split, :, :, :, :, lanes(t % split)]))
-    half, slot = tile_place(8 * split)
+    for out, matrix, index in (
+            [(d_lat_out, LATENTS_AT + i, i) for i in range(SIDE)] + [(w_out_grads, QUERY_AT, 0)]
+            + [(w_out_grads, MLP_AT + i, i + 1) for i in range(3)] + [(kv_out, KEY_AT, 0), (kv_out, VALUE_AT, 1)]):
+        for t in range(split):
+            half, slot = tile_place(matrix, t)
+            outs.append(fetch(g.at[half, :, :, :, slot], out.at[index, :, :, :, :, lanes(t)]))
+    half, slot = tile_place(KEY_AT, 0)
     outs.append(fetch(g.at[half, SIDE - 1, :, :, slot], vec_out))
     for copy in forwarded + list(ring.values()):
         copy.wait_recv()
@@ -734,6 +748,44 @@
     )(q, k, v, d_attn, z_all, *others)
 
 
+def finish_kernel(z_in, lat_in, w_in, kv_in, z_out, lat_out, wq, wo, wu, wd, wk, wv, z_buf, lat_buf, w_buf, sems):
+    local = LocalCopies(sems)
+    moves = []
+    w_outs = (wq, wo, wu, wd)
+    for i in range(z_buf.shape[0]):
+        moves.append((local.start(z_in.at[i], z_buf.at[i]), z_buf.at[i], z_out.at[i]))
+        if i < SIDE:
+            moves.append((local.start(lat_in.at[i], lat_buf.at[i]), lat_buf.at[i], lat_out.at[i]))
+            moves.append((local.start(w_in.at[i], w_buf.at[i]), w_buf.at[i], w_outs[i]))
+    written = []
+    for copy, src, dst in moves:
+        copy.wait()
+        written.append(local.start(src, dst))
+    rows = wk.shape[0]
+    wk[...] = kv_in[0, 0:rows, :]
+    wv[...] = kv_in[1, 0:rows, :]
+    for copy in written:
+        copy.wait()
+
+
+def finish(z_all, d_lat, w_sums, kv_sums, channels):
+    vmem = pl.BlockSpec(memory_space=pltpu.VMEM)
+    hbm = pl.BlockSpec(memory_space=pl.ANY)
+    shape = jax.ShapeDtypeStruct
+    width = w_sums.shape[-1]
+    square = shape((width, width), F32)
+    tall = shape((channels, width), F32)
+    return pl.pallas_call(
+        finish_kernel,
+        out_shape=(shape(z_all.shape, F32), shape(d_lat.shape, F32), square, square, square, square, tall, tall),
+        in_specs=[hbm] * 3 + [vmem],
+        out_specs=(hbm,) * 6 + (vmem,) * 2,
+        scratch_shapes=[pltpu.VMEM(z_all.shape, F32), pltpu.VMEM(d_lat.shape, F32), pltpu.VMEM(w_sums.shape, F32),
+                        pltpu.SemaphoreType.DMA((64,))],
+        compiler_params=pltpu.CompilerParams(vmem_limit_bytes=VMEM_LIMIT),
+    )(z_all, d_lat, w_sums, kv_sums)
+
+
 def solution(mesh):
     x_spec = P('dp', 'cp', None)
     row_spec = P('dp', None, None)
@@ -759,12 +811,13 @@
         z_all, d_inputs, d_lat, w_sums, kv_sums, vec_sums = backward_block(
             q, k, v, d_attn.reshape(n_latents, width), z_all, stats, top, d_mid, vec_grads, *norms,
             w_grads.reshape(3, SIDE, SIDE, SIDE, 8, width), x_in, latents, collective_id=1)
-        w_sums = w_sums.reshape(4, width, width)
-        kv_sums = kv_sums.reshape(2, width, width)[:, :channels]
+        z_out, d_lat, d_w_query, d_w_out, d_w_up, d_w_down, d_w_key, d_w_value = finish(
+            z_all.reshape(PLANE, -1, width), d_lat.reshape(SIDE, -1, width), w_sums.reshape(SIDE, width, width),
+            kv_sums.reshape(2, width, width), channels)
         vec_sums = vec_sums[:2, :, :width // LANES].reshape(2 * SIDE, width)
-        return (z_all.reshape(batch, n_latents, width), d_inputs.transpose(0, 2, 1), d_lat.reshape(n_latents, width),
+        return (z_out.reshape(batch, n_latents, width), d_inputs.transpose(0, 2, 1), d_lat.reshape(n_latents, width),
                 vec_sums[6, :channels], vec_sums[7, :channels], vec_sums[4], vec_sums[5],
-                w_sums[0], kv_sums[0], kv_sums[1], w_sums[1], vec_sums[0], vec_sums[1],
-                w_sums[2], vec_sums[2], w_sums[3], vec_sums[3])
+                d_w_query, d_w_key, d_w_value, d_w_out, vec_sums[0], vec_sums[1],
+                d_w_up, vec_sums[2], d_w_down, vec_sums[3])
 
     return jax.shard_map(local_step, mesh=mesh, in_specs=in_specs, out_specs=out_specs, check_vma=False)

time: 271 us -> 259 us (0.956)
  local copies, waits for them, and re-layouts: 27.5 us -> 6.64 us
  Pallas kernels: 240 us -> 249 us
    pallas_call x0 -> x1, Pallas kernels: none -> 20.3 us  [finish(): pl.pallas_call(finish_kernel, out_shape=(shape(z_all.shape, F32), shape(d...]
    unnamed x6 -> x2, local copies, waits for them, and re-layouts: 16.1 us -> 2.19 us
    pallas_call x1, Pallas kernels: 147 us -> 136 us  [backward_block(): pl.pallas_call(backward_kernel, out_shape=(shape(z_all.shape, F32), shape...]
    slice x1 -> x0, local copies, waits for them, and re-layouts: 4.47 us -> none  [local_step(): w_sums[3]]
where the time goes in v3:
time: 259 us
  Pallas kernels  249 us (96%)
  local copies, waits for them, and re-layouts  6.64 us (3%)
    pallas_call x1, Pallas kernels, backward_block(): pl.pallas_call(backward_kernel, out_shape=(shape(z_all.shape, F32), shape...  136 us
    pallas_call x1, Pallas kernels, forward_block(): pl.pallas_call(forward_kernel, out_shape=tuple((shape(*one) for one in sa...  92.7 us
    pallas_call x1, Pallas kernels, finish(): pl.pallas_call(finish_kernel, out_shape=(shape(z_all.shape, F32), shape(d...  20.3 us

profile of v3, /device:TPU:1, one launch (start us, length us, event | category | flops | bytes accessed | tf_op | source)
XLA Modules:
  0.0 258.7 jit_solution(6457186839623217865)
XLA Ops:
  0.7 1.2 reshape.85.x_gain_row
  1.9 1.2 reshape.86.x_shift_row
  3.1 2.3 convert_bitcast_fusion.x_blocks
  5.4 92.7 %shard_map.296 = (bf16[2048,512]{1,0:T(8,128)(2,1)}, bf16[1024,512]{1,0:T(8,128)(2,1)}, bf16[1024,512]{1,0:T(8,128)(2,1)}, f32[4,322,256]{2,1,0:T(8,128)}, f32[4...) custom-call(f32[4,322,256]{2,1,0:T(8,128)} %convert_bitcast_fusion.x, ...), custom_call_target="tpu_custom_call" | custom-call | tf_op jit(solution)/shard_map/pallas_call | solution.py:380
  98.1 136.1 %shard_map.297 = (f32[4,4,4,128,512]{4,3,2,1,0:T(8,128)}, bf16[4,322,256]{2,1,0:T(8,128)(2,1)}, f32[4,4,4,4,8,512]{5,4,3,2,1,0:T(8,128)}, f32[4,4,4,4,8,512]{5,4...) custom-call(bf16[2048,512]{1,0:T(8,128)(2,1)} %get-tuple-element.42., ...), custom_call_target="tpu_custom_call", output_to_operand_aliasing={{0}: (4, {})} | custom-call | tf_op jit(solution)/shard_map/pallas_call | solution.py:737
  234.2 20.3 %shard_map.298 = (f32[16,512,512]{2,1,0:T(8,128)}, f32[4,512,512]{2,1,0:T(8,128)}, f32[512,512]{1,0:T(8,128)}, f32[512,512]{1,0:T(8,128)}, f32[512,512]{1,0:T(8,...) custom-call(f32[16,512,512]{2,1,0:T(8,128)} %bitcast.28, f32[4,512,512]{2,1,0:T(8,128)} %bitcast.29, ...), custom_call_target="tpu_custom_call" | custom-call | tf_op jit(solution)/shard_map/pallas_call | solution.py:778
  254.6 0.8 slice.27
  255.3 0.6 slice_reduce_fusion
  255.9 0.6 fusion
  256.5 2.2 copy.36
  (1 shorter events, 0.0 us)

commit v4 on v3

--- a/solution.py
+++ b/solution.py
@@ -16,6 +16,7 @@
 PLANE = SIDE * SIDE
 LANES = 128
 LATENT_TILE = 256
+RELAY_ROWS = 160
 LOG2E = math.log2(math.e)
 GELU_C = math.sqrt(2.0 / math.pi)
 GELU_A = 0.044715
@@ -39,6 +40,7 @@
 TN = ((0,), (0,))
 DOWN, ACROSS = 0, 1
 HOPS = (2, 1, 3)
+WAYS = (1, -1)
 
 
 def mean(value, axis=ACROSS):
@@ -72,8 +74,9 @@
     return rstd * (d_unit - mean(d_unit, axis) - unit * mean(d_unit * unit, axis))
 
 
-def as_column(row):
-    return jnp.broadcast_to(row[...], (LANES, row.shape[1])).T[:, :1]
+def as_columns(rows):
+    turned = jnp.concatenate([rows[...], zeros(LANES - rows.shape[0], rows.shape[1])], axis=DOWN).T
+    return turned[:, :1], turned[:, 1:2]
 
 
 def row_pair(ref, i):
@@ -156,14 +159,39 @@
     return {'zyx'[axis]: value}
 
 
+class SwapZ:
+    def __init__(self, copies, me, src, dst, relays):
+        self.copies, self.me, self.dst, self.relays = copies, me, dst, relays
+        far = moved(me, 0, 2)[0]
+        cut = relays[0].shape[0]
+        self.parts = (pl.ds(0, cut), pl.ds(cut, src.shape[1] - cut))
+        self.halves = [copies.start(src.at[far, part], relay, chip(*moved(me, 0, d)))
+                       for d, part, relay in zip(WAYS, self.parts, relays)]
+        self.src = src
+
+    def near(self):
+        self.blocks = []
+        for d in WAYS:
+            peer = moved(self.me, 0, d)
+            self.blocks.append(self.copies.start(self.src.at[peer[0]], self.dst.at[self.me[0]], chip(*peer)))
+
+    def forward(self):
+        self.rest = []
+        for d, part, relay, half in zip(WAYS, self.parts, self.relays, self.halves):
+            half.wait_recv()
+            origin = moved(self.me, 0, -d)[0]
+            self.rest.append(self.copies.start(relay, self.dst.at[origin, part], chip(*moved(self.me, 0, d))))
+
+
 def forward_kernel(
-        x_blocks, latents_in, d_out_in, x_gain_row, x_shift_row, z_gain, z_shift, w_query, w_key, w_value,
-        w_out, w_up, w_down, m_gain, m_shift, b_up, b_down,
+        x_blocks, latents_in, d_out_in, x_affine, z_gain, z_shift, w_query, w_key, w_value,
+        w_out_in, w_up_in, w_down_in, m_gain, m_shift, b_up, b_down,
         q_out, k_out, v_out, x_out, z_all, w_grads_out, d_attn_all, stats_all, top_all, d_mid_out, vec_grads,
-        q, k, v, x_in, latents, d_out, z_out, w_grads,
+        q, k, v, x_in, latents, d_out, z_out, w_grads, w_out, w_up, w_down, relay_up, relay_down,
         vt, logits, mixed, top_own, tops, sum_own, sum_parts, sums, sa, sb, fa, fb, pa1, pb1, ra2, rb2, d_attn_f32, stats_f32,
         send_sems, recv_sems, local_sems):
     me = chip_coords()
+    relays = (relay_up, relay_down)
     local = LocalCopies(local_sems)
     got_latents = local.start(latents_in, latents)
     got_own = local.start(x_blocks.at[me[0]], x_in.at[me[0]])
@@ -176,21 +204,19 @@
     enter([device for _, device in plane_peers] + [chip(*moved(me, 0, d)) for d in HOPS])
     copies = Copies(send_sems, recv_sems)
     chunk = d_out.shape[0]
+    got_w = [local.start(*pair) for pair in ((w_out_in, w_out), (w_up_in, w_up), (w_down_in, w_down))]
     got_d_out = local.start(d_out_in.at[z, pl.ds(owner * chunk, chunk), :], d_out)
     qk_scale = q.shape[1] ** -0.5
     to_log2 = qk_scale * LOG2E
     tiles = q.shape[0] // LATENT_TILE
     halves = (slice(0, SIDE // 2), slice(SIDE // 2, SIDE))
-    ways = (1, -1)
     half_v = vt.shape[0] // 2
     block_rows = x_blocks.shape[-1]
 
-    got_x = {}
-    for d in HOPS:
-        peer = moved(me, 0, d)
-        got_x[d] = copies.start(x_blocks.at[peer[0]], x_in.at[z], chip(*peer))
+    swap = SwapZ(copies, me, x_blocks, x_in, relays)
+    swap.near()
     top_own[...] = jnp.full(top_own.shape, -jnp.inf, F32)
-    x_gain, x_shift = as_column(x_gain_row), as_column(x_shift_row)
+    x_gain, x_shift = as_columns(x_affine)
     got_latents.wait()
 
     def query_tile(i, carry):
@@ -224,9 +250,13 @@
         lax.fori_loop(0, tiles, logits_tile, 0)
 
     block_logits(z)
-    for d in HOPS[::-1]:
-        got_x[d].wait_recv()
+    swap.forward()
+    for d, copy in zip(WAYS, swap.blocks):
+        copy.wait_recv()
         block_logits(moved(me, 0, -d)[0])
+    for copy in swap.rest:
+        copy.wait_recv()
+    block_logits(moved(me, 0, 2)[0])
     top_own[...] = jnp.ceil(top_own[...] * to_log2)
     saved += [local.start(k, k_out), local.start(v, v_out), local.start(x_in, x_out)]
     tops[owner] = top_own[...]
@@ -264,13 +294,13 @@
     for axis, _, cols, side_in, _, _, _ in streams:
         far = moved(me, axis, 2)[axis]
         first.append([copies.start(mixed.at[mixed_at(axis, far, halves[w], cols)], side_in.at[w], chip(*moved(me, axis, d)))
-                      for w, d in enumerate(ways)])
+                      for w, d in enumerate(WAYS)])
     sums[owner] = sum_parts[owner]
     sum_copies = [copies.start(sum_parts.at[other], sums.at[owner], device) for other, device in plane_peers]
     full = []
     for (axis, _, cols, side_in, full_in, _, _), arriving in zip(streams, first):
         started = []
-        for w, d in enumerate(ways):
+        for w, d in enumerate(WAYS):
             peer = moved(me, axis, d)
             arriving[w].wait_recv()
             mixed[mixed_at(axis, peer[axis], halves[w], cols)] += side_in[w]
@@ -295,6 +325,8 @@
     attn_t = jnp.concatenate([upper, lower], axis=DOWN) * inv_sum[0:1, :]
 
     attn_t_low = attn_t.astype(BF16)
+    for copy in got_w:
+        copy.wait()
     attn_low = attn_t.T.astype(BF16)
     z_mid = latents[tile_rows(owner, chunk), :] + dot(attn_low, w_out[...], NN)
     unit, rstd = norm_parts(z_mid)
@@ -348,10 +380,10 @@
         for copy in arriving:
             copy.wait_recv()
         ref = d_attn_f32.at[mixed_at(axis, me[axis], slice(None), rows)]
-        gathered.append((axis, rows, [copies.start(ref, ref, chip(*moved(me, axis, d))) for d in ways]))
+        gathered.append((axis, rows, [copies.start(ref, ref, chip(*moved(me, axis, d))) for d in WAYS]))
     last = []
     for axis, rows, arriving in gathered:
-        for w, d in enumerate(ways):
+        for w, d in enumerate(WAYS):
             arriving[w].wait_recv()
             ref = d_attn_f32.at[mixed_at(axis, moved(me, axis, -d)[axis], halves[w], rows)]
             last.append(copies.start(ref, ref, chip(*moved(me, axis, d))))
@@ -382,10 +414,12 @@
         out_shape=tuple(shape(*one) for one in saved) + (
             shape((SIDE, SIDE, SIDE, chunk, width), F32), shape((3, width, width), F32), shape((PLANE, chunk, width), BF16),
             shape(stat, F32), shape((PLANE, LANES), F32), shape((chunk, width), F32), shape((8, width), F32)),
-        in_specs=[hbm] * 3 + [vmem] * len(others),
+        in_specs=[hbm] * 3 + [vmem] * (len(others) - 7) + [hbm] * 3 + [vmem] * 4,
         out_specs=(hbm,) * 6 + (vmem,) * 5,
         scratch_shapes=[wide(*one) for one in saved] + [
             wide((latents_n, width), F32), wide((chunk, width), BF16), wide((chunk, width), F32), wide((3, width, width), F32),
+            wide((width, width), BF16), wide((width, width), BF16), wide((width, width), BF16),
+            wide((RELAY_ROWS, block_rows), F32), wide((channels - RELAY_ROWS, block_rows), F32),
             wide((width, elements), BF16), wide((latents_n // LATENT_TILE, elements, LATENT_TILE), F32),
             wide((SIDE, SIDE, width, LANES), F32),
             wide((PLANE, LANES), F32), wide((PLANE, PLANE, LANES), F32), wide((PLANE, LANES), F32), wide(stat, F32), wide(stat, F32),
@@ -407,10 +441,11 @@
 
 
 def backward_kernel(
-        q_in, k_in, v_in, d_attn_in, z_in, stats, top, d_mid, vec_grads, x_gain_row, x_shift_row, z_gain, z_shift,
+        q_in, k_in, v_in, d_attn_in, z_in, stats, top, d_mid, vec_grads, x_affine, z_gain, z_shift,
         w_query, w_key, w_value, w_grads, x_in, latents_in,
         z_all, d_inputs, d_lat_out, w_out_grads, kv_out, vec_out,
-        q, k, v, d_attn, probs, d_logits, d_q, d_k, d_v, x_rows, x_norm, x_sums, d_x, d_x_in, latents, z_norm, vecs, g, core_in, *rest):
+        q, k, v, d_attn, probs, d_logits, d_q, d_k, d_v, x_rows, x_norm, x_sums, d_x, d_x_in, relay_up, relay_down, latents, z_norm, vecs, g, core_in, *rest):
+    relays = (relay_up, relay_down)
     n, per = len(STREAM_TILES), 8
     side_in = [rest[per * s:per * s + 2] for s in range(n)]
     full_in = [rest[per * s + 2:per * s + 4] for s in range(n)]
@@ -436,11 +471,10 @@
     enter([partner] + [chip(*moved(me, axis, d)) for axis in range(3) for d in HOPS])
     copies = Copies(send_sems, recv_sems)
 
-    ways = (1, -1)
     z_pending = []
     for (lo, hi), (first, second, _) in zip(STREAM_ROWS, STREAM_AXES):
         ref = z_all.at[at((first,), me) + (pl.ds(lo, hi - lo),)]
-        z_pending.append([copies.start(ref, ref, chip(*moved(me, second, d))) for d in ways])
+        z_pending.append([copies.start(ref, ref, chip(*moved(me, second, d))) for d in WAYS])
     got_x = fetch(x_in, x_rows)
     got_latents = fetch(latents_in, latents)
     got_w = []
@@ -449,7 +483,7 @@
             half, slot = tile_place(MLP_AT + i, t)
             got_w.append(fetch(w_grads.at[i, :, :, :, :, lanes(t)], g.at[half, :, :, :, slot]))
     x_norm[...] = jnp.zeros(x_norm.shape, BF16)
-    x_gain, x_shift = as_column(x_gain_row), as_column(x_shift_row)
+    x_gain, x_shift = as_columns(x_affine)
     for copy in got_first:
         copy.wait()
 
@@ -472,7 +506,7 @@
     for s, (lo, hi) in enumerate(STREAM_ROWS):
         first, second, _ = STREAM_AXES[s]
         arrived, z_pending[s] = z_pending[s], []
-        for copy, d, part in zip(arrived, ways, halves):
+        for copy, d, part in zip(arrived, WAYS, halves):
             copy.wait_recv()
             origin = on(second, moved(me, second, -d)[second])
             ref = z_all.at[at((), me, **on(first, part), **origin) + (pl.ds(lo, hi - lo),)]
@@ -544,10 +578,7 @@
         return carry
 
     lax.fori_loop(0, SIDE, element_tile, 0)
-    x_pending = []
-    for d in HOPS:
-        peer = moved(me, 0, d)
-        x_pending.append(copies.start(d_x.at[peer[0]], d_x_in.at[z], chip(*peer)))
+    swap = SwapZ(copies, me, d_x, d_x_in, relays)
     d_x_in[z] = d_x[z]
 
     for h in range(2):
@@ -591,7 +622,6 @@
         for t in range(split):
             g[half, SIDE - 1, i // SIDE, i % SIDE, slot, t:t + 1, :] = vecs[i:i + 1, t * LANES:(t + 1) * LANES]
     exchange(2)
-    start_ring(2)
 
     for copy, (lo, hi) in zip(exchanged, SLOT_GROUPS):
         copy.wait_recv()
@@ -616,18 +646,20 @@
     for s in range(n):
         axis = STREAM_AXES[s][0]
         far = moved(me, axis, 2)[axis]
-        first.append([send(along(s, far, halves[w]), None, side_in[s][w], moved(me, axis, d)) for w, d in enumerate(ways)])
-    start_ring(3)
+        first.append([send(along(s, far, halves[w]), None, side_in[s][w], moved(me, axis, d)) for w, d in enumerate(WAYS)])
+    swap.near()
+    start_ring(2)
     pending = []
     for s in range(n):
         axis = STREAM_AXES[s][0]
         started = []
-        for w, d in enumerate(ways):
+        for w, d in enumerate(WAYS):
             peer = moved(me, axis, d)
             first[s][w].wait_recv()
             g[along(s, peer[axis], halves[w])] += side_in[s][w][...]
             started.append(send(along(s, peer[axis]), None, full_in[s][w], peer))
         pending.append(started)
+    start_ring(3)
     for phase in range(1, 3):
         for s in range(n):
             for copy in pending[s]:
@@ -650,6 +682,8 @@
                 index = tuple(peer[axis] if a == axis else slice(None) for a in left)
                 started.append(copies.start(part.at[index], recvs[s][phase].at[d - 1], chip(*peer)))
             pending[s] = started
+        if phase == 1:
+            swap.forward()
         forward_ring(phase - 1)
     for s, (lo, hi) in enumerate(STREAM_TILES):
         for copy in pending[s]:
@@ -676,16 +710,16 @@
             copy.wait_recv()
         axis = STREAM_AXES[s][0]
         index = along(s, me[axis])
-        pending[s] = [send(index, index, None, moved(me, axis, d)) for d in ways]
+        pending[s] = [send(index, index, None, moved(me, axis, d)) for d in WAYS]
         to_partner(index)
-    for copy in x_pending:
+    for copy in swap.blocks + swap.rest:
         copy.wait_recv()
     for i in range(SIDE):
         d_inputs[i] = d_x_in[i].astype(BF16)
     last = []
     for s in range(n):
         axis = STREAM_AXES[s][0]
-        for w, d in enumerate(ways):
+        for w, d in enumerate(WAYS):
             pending[s][w].wait_recv()
             index = along(s, moved(me, axis, -d)[axis], halves[w])
             last.append((send(index, index, None, moved(me, axis, d)), s, w))
@@ -726,6 +760,7 @@
         wide(q.shape, BF16), wide(k.shape, BF16), wide(v.shape, BF16), wide(q.shape, BF16), wide((elements, n_latents), BF16), wide((elements, n_latents), BF16),
         wide((n_latents, width), BF16), wide((elements, width), BF16), wide((elements, width), BF16),
         wide(block, F32), wide((width, elements), BF16), wide((2, channels, LANES), F32), wide(block, F32), wide(block, F32),
+        wide((RELAY_ROWS, block[-1]), F32), wide((channels - RELAY_ROWS, block[-1]), F32),
         wide((n_latents, width), F32), wide((n_latents, width), BF16), wide((8, width), F32),
         wide((2,) + cube + (HALF_TILES, 8, LANES), F32), wide(cube + (HALF_TILES, 8, LANES), F32)]
     for lo, hi in STREAM_TILES:
@@ -748,7 +783,9 @@
     )(q, k, v, d_attn, z_all, *others)
 
 
-def finish_kernel(z_in, lat_in, w_in, kv_in, z_out, lat_out, wq, wo, wu, wd, wk, wv, z_buf, lat_buf, w_buf, sems):
+def finish_kernel(z_in, lat_in, w_in, kv_in, x_in, vec_in,
+                  z_out, lat_out, wq, wo, wu, wd, wk, wv, x_out, *rest):
+    vec_outs, (z_buf, lat_buf, w_buf, sems) = rest[:-SIDE], rest[-SIDE:]
     local = LocalCopies(sems)
     moves = []
     w_outs = (wq, wo, wu, wd)
@@ -762,28 +799,36 @@
         copy.wait()
         written.append(local.start(src, dst))
     rows = wk.shape[0]
+    for i in range(SIDE):
+        x_out[:, i, :] = x_in[i]
+    for i, out in enumerate(vec_outs):
+        line = jnp.concatenate([vec_in[i // SIDE, i % SIDE, t:t + 1, :] for t in range(wk.shape[1] // LANES)], axis=ACROSS)
+        out[...] = line[:, :out.shape[1]]
     wk[...] = kv_in[0, 0:rows, :]
     wv[...] = kv_in[1, 0:rows, :]
     for copy in written:
         copy.wait()
 
 
-def finish(z_all, d_lat, w_sums, kv_sums, channels):
+def finish(z_all, d_lat, w_sums, kv_sums, d_x, vec_sums):
     vmem = pl.BlockSpec(memory_space=pltpu.VMEM)
     hbm = pl.BlockSpec(memory_space=pl.ANY)
     shape = jax.ShapeDtypeStruct
     width = w_sums.shape[-1]
     square = shape((width, width), F32)
+    _, channels, columns = d_x.shape
     tall = shape((channels, width), F32)
+    line, x_line = shape((1, width), F32), shape((1, channels), F32)
     return pl.pallas_call(
         finish_kernel,
-        out_shape=(shape(z_all.shape, F32), shape(d_lat.shape, F32), square, square, square, square, tall, tall),
-        in_specs=[hbm] * 3 + [vmem],
-        out_specs=(hbm,) * 6 + (vmem,) * 2,
+        out_shape=(shape(z_all.shape, F32), shape(d_lat.shape, F32), square, square, square, square, tall, tall,
+                   shape((channels, SIDE, columns), BF16)) + (line,) * 6 + (x_line,) * 2,
+        in_specs=[hbm] * 3 + [vmem] * 3,
+        out_specs=(hbm,) * 6 + (vmem,) * 11,
         scratch_shapes=[pltpu.VMEM(z_all.shape, F32), pltpu.VMEM(d_lat.shape, F32), pltpu.VMEM(w_sums.shape, F32),
                         pltpu.SemaphoreType.DMA((64,))],
         compiler_params=pltpu.CompilerParams(vmem_limit_bytes=VMEM_LIMIT),
-    )(z_all, d_lat, w_sums, kv_sums)
+    )(z_all, d_lat, w_sums, kv_sums, d_x, vec_sums)
 
 
 def solution(mesh):
@@ -805,19 +850,18 @@
 
         x_blocks = inputs.transpose(0, 2, 1).astype(F32)
         row = lambda vec: vec.reshape(1, -1)
-        norms = (row(x_gain), row(x_shift), row(z_gain), row(z_shift), w_query, w_key, w_value)
+        norms = (jnp.stack([x_gain, x_shift]), row(z_gain), row(z_shift), w_query, w_key, w_value)
         q, k, v, x_in, z_all, w_grads, d_attn, stats, top, d_mid, vec_grads = forward_block(
             x_blocks, latents, d_out, *norms, w_out, w_up, w_down, row(m_gain), row(m_shift), row(b_up), row(b_down), collective_id=0)
         z_all, d_inputs, d_lat, w_sums, kv_sums, vec_sums = backward_block(
             q, k, v, d_attn.reshape(n_latents, width), z_all, stats, top, d_mid, vec_grads, *norms,
             w_grads.reshape(3, SIDE, SIDE, SIDE, 8, width), x_in, latents, collective_id=1)
-        z_out, d_lat, d_w_query, d_w_out, d_w_up, d_w_down, d_w_key, d_w_value = finish(
+        z_out, d_lat, d_w_query, d_w_out, d_w_up, d_w_down, d_w_key, d_w_value, d_inputs, *vectors = finish(
             z_all.reshape(PLANE, -1, width), d_lat.reshape(SIDE, -1, width), w_sums.reshape(SIDE, width, width),
-            kv_sums.reshape(2, width, width), channels)
-        vec_sums = vec_sums[:2, :, :width // LANES].reshape(2 * SIDE, width)
-        return (z_out.reshape(batch, n_latents, width), d_inputs.transpose(0, 2, 1), d_lat.reshape(n_latents, width),
-                vec_sums[6, :channels], vec_sums[7, :channels], vec_sums[4], vec_sums[5],
-                d_w_query, d_w_key, d_w_value, d_w_out, vec_sums[0], vec_sums[1],
-                d_w_up, vec_sums[2], d_w_down, vec_sums[3])
+            kv_sums.reshape(2, width, width), d_inputs, vec_sums)
+        d_m_gain, d_m_shift, d_b_up, d_b_down, d_z_gain, d_z_shift, d_x_gain, d_x_shift = [v.reshape(-1) for v in vectors]
+        return (z_out.reshape(batch, n_latents, width), d_inputs.transpose(1, 2, 0), d_lat.reshape(n_latents, width),
+                d_x_gain, d_x_shift, d_z_gain, d_z_shift, d_w_query, d_w_key, d_w_value, d_w_out, d_m_gain, d_m_shift,
+                d_w_up, d_b_up, d_w_down, d_b_down)
 
     return jax.shard_map(local_step, mesh=mesh, in_specs=in_specs, out_specs=out_specs, check_vma=False)

time: 259 us -> 259 us (level)
  local copies, waits for them, and re-layouts: 6.64 us -> 1.37 us
  other arithmetic: 2.25 us -> 5.38 us
    pallas_call x1, Pallas kernels: 136 us -> 139 us  [backward_block(): pl.pallas_call(backward_kernel, out_shape=(shape(z_all.shape, F32), shape...]
where the time goes in v4:
time: 259 us
  Pallas kernels  251 us (97%)
  other arithmetic  5.38 us (2%)
    pallas_call x1, Pallas kernels, backward_block(): pl.pallas_call(backward_kernel, out_shape=(shape(z_all.shape, F32), shape...  139 us
    pallas_call x1, Pallas kernels, forward_block(): pl.pallas_call(forward_kernel, out_shape=tuple((shape(*one) for one in sa...  91.3 us
    pallas_call x1, Pallas kernels, finish(): pl.pallas_call(finish_kernel, out_shape=(shape(z_all.shape, F32), shape(d...  21.3 us

profile of v4, /device:TPU:1, one launch (start us, length us, event | category | flops | bytes accessed | tf_op | source)
XLA Modules:
  0.0 258.8 jit_solution(2119369163026165223)
XLA Ops:
  0.7 0.7 stack.9
  1.3 0.7 stack.10
  2.0 0.6 pad_maximum_fusion.x_affine
  2.6 2.3 convert_bitcast_fusion.x_blocks
  4.9 91.3 %shard_map.296 = (bf16[2048,512]{1,0:T(8,128)(2,1)}, bf16[1024,512]{1,0:T(8,128)(2,1)}, bf16[1024,512]{1,0:T(8,128)(2,1)}, f32[4,322,256]{2,1,0:T(8,128)}, f32[4...) custom-call(f32[4,322,256]{2,1,0:T(8,128)} %convert_bitcast_fusion.x, ...), custom_call_target="tpu_custom_call" | custom-call | tf_op jit(solution)/shard_map/pallas_call | solution.py:412
  96.2 138.7 %shard_map.297 = (f32[4,4,4,128,512]{4,3,2,1,0:T(8,128)}, bf16[4,322,256]{2,1,0:T(8,128)(2,1)}, f32[4,4,4,4,8,512]{5,4,3,2,1,0:T(8,128)}, f32[4,4,4,4,8,512]{5,4...) custom-call(bf16[2048,512]{1,0:T(8,128)(2,1)} %get-tuple-element.51., ...), custom_call_target="tpu_custom_call", output_to_operand_aliasing={{0}: (4, {})} | custom-call | tf_op jit(solution)/shard_map/pallas_call | solution.py:772
  234.9 21.3 %shard_map.298 = (f32[16,512,512]{2,1,0:T(8,128)}, f32[4,512,512]{2,1,0:T(8,128)}, f32[512,512]{1,0:T(8,128)}, f32[512,512]{1,0:T(8,128)}, f32[512,512]{1,0:T(8,...) custom-call(f32[16,512,512]{2,1,0:T(8,128)} %bitcast.23, ...), custom_call_target="tpu_custom_call" | custom-call | tf_op jit(solution)/shard_map/pallas_call | solution.py:822
  256.2 1.3 reduce
  257.5 1.3 reduce.1

commit v5 on v4

--- a/solution.py
+++ b/solution.py
@@ -579,6 +579,7 @@
 
     lax.fori_loop(0, SIDE, element_tile, 0)
     swap = SwapZ(copies, me, d_x, d_x_in, relays)
+    swap.near()
     d_x_in[z] = d_x[z]
 
     for h in range(2):
@@ -622,6 +623,7 @@
         for t in range(split):
             g[half, SIDE - 1, i // SIDE, i % SIDE, slot, t:t + 1, :] = vecs[i:i + 1, t * LANES:(t + 1) * LANES]
     exchange(2)
+    start_ring(2)
 
     for copy, (lo, hi) in zip(exchanged, SLOT_GROUPS):
         copy.wait_recv()
@@ -647,8 +649,7 @@
         axis = STREAM_AXES[s][0]
         far = moved(me, axis, 2)[axis]
         first.append([send(along(s, far, halves[w]), None, side_in[s][w], moved(me, axis, d)) for w, d in enumerate(WAYS)])
-    swap.near()
-    start_ring(2)
+    start_ring(3)
     pending = []
     for s in range(n):
         axis = STREAM_AXES[s][0]
@@ -659,7 +660,6 @@
             g[along(s, peer[axis], halves[w])] += side_in[s][w][...]
             started.append(send(along(s, peer[axis]), None, full_in[s][w], peer))
         pending.append(started)
-    start_ring(3)
     for phase in range(1, 3):
         for s in range(n):
             for copy in pending[s]:

time: 259 us -> 254 us (0.981)
  Pallas kernels: 251 us -> 246 us
    pallas_call x1, Pallas kernels: 139 us -> 133 us  [backward_block(): pl.pallas_call(backward_kernel, out_shape=(shape(z_all.shape, F32), shape...]
where the time goes in v5:
time: 254 us; the launch traced here: 253 us
  Pallas kernels  246 us (97%)
  other arithmetic  5.38 us (2%)
    pallas_call x1, Pallas kernels, backward_block(): pl.pallas_call(backward_kernel, out_shape=(shape(z_all.shape, F32), shape...  133 us
    pallas_call x1, Pallas kernels, forward_block(): pl.pallas_call(forward_kernel, out_shape=tuple((shape(*one) for one in sa...  91.3 us
    pallas_call x1, Pallas kernels, finish(): pl.pallas_call(finish_kernel, out_shape=(shape(z_all.shape, F32), shape(d...  21.3 us

profile of v5, /device:TPU:1, one launch (start us, length us, event | category | flops | bytes accessed | tf_op | source)
XLA Modules:
  0.0 253.4 jit_solution(763228068375515932)
XLA Ops:
  0.7 0.7 stack.9
  1.3 0.7 stack.10
  2.0 0.6 pad_maximum_fusion.x_affine
  2.6 2.3 convert_bitcast_fusion.x_blocks
  4.9 91.3 %shard_map.296 = (bf16[2048,512]{1,0:T(8,128)(2,1)}, bf16[1024,512]{1,0:T(8,128)(2,1)}, bf16[1024,512]{1,0:T(8,128)(2,1)}, f32[4,322,256]{2,1,0:T(8,128)}, f32[4...) custom-call(f32[4,322,256]{2,1,0:T(8,128)} %convert_bitcast_fusion.x, ...), custom_call_target="tpu_custom_call" | custom-call | tf_op jit(solution)/shard_map/pallas_call | solution.py:412
  96.2 133.3 %shard_map.297 = (f32[4,4,4,128,512]{4,3,2,1,0:T(8,128)}, bf16[4,322,256]{2,1,0:T(8,128)(2,1)}, f32[4,4,4,4,8,512]{5,4,3,2,1,0:T(8,128)}, f32[4,4,4,4,8,512]{5,4...) custom-call(bf16[2048,512]{1,0:T(8,128)(2,1)} %get-tuple-element.51., ...), custom_call_target="tpu_custom_call", output_to_operand_aliasing={{0}: (4, {})} | custom-call | tf_op jit(solution)/shard_map/pallas_call | solution.py:772
  229.5 21.3 %shard_map.298 = (f32[16,512,512]{2,1,0:T(8,128)}, f32[4,512,512]{2,1,0:T(8,128)}, f32[512,512]{1,0:T(8,128)}, f32[512,512]{1,0:T(8,128)}, f32[512,512]{1,0:T(8,...) custom-call(f32[16,512,512]{2,1,0:T(8,128)} %bitcast.23, ...), custom_call_target="tpu_custom_call" | custom-call | tf_op jit(solution)/shard_map/pallas_call | solution.py:822
  250.8 1.3 reduce
  252.1 1.3 reduce.1
